TPU v7x, 128 devices: a whole 4x4x4 slice. The times are simulated.
128 devices in a mesh: row: 8 (over z, y_lo), col: 16 (over y_hi, x, core).
Axes of the slice: x: 4, y: 4 (y_hi: 2, y_lo: 2; y = y_hi * 2 + y_lo), z: 4, core: 2. Of those that a mesh axis runs over, the one named last changes fastest.
Arguments:
- joined_weight: bfloat16 [16, 2880, 5760], P('row', 'col'), may hold values from -0.109375 to 0.109375
- tile_perm: int32 [144], replicated, may hold values from 0 to 143, each once
- down_weight: bfloat16 [16, 2880, 2880], P('row', 'col'), may hold values from -0.109375 to 0.109375
- tokens: bfloat16 [1024, 2880], P(('row', 'col')), may hold values from -6 to 6
- expert_ids: int32 [1024, 4], replicated, may hold values from 0 to 15, all different within a row; in each aligned block of 1024 rows (0 to 1023, 1024 to 2047, ...) at most 512 rows name the same one
- route_scores: float32 [1024, 4], replicated, may hold values from 0.1 to 1
Outputs:
- gate_weight: bfloat16 [16, 2880, 2880], P('row', None, 'col')
- up_weight: bfloat16 [16, 2880, 2880], P('row', None, 'col')
- mixed: bfloat16 [1024, 2880], P(('row', 'col'))
Inputs may be any that keep to these rules, and one draw needn't show every extreme that they name: `expert_ids`: every expert is chosen by at most 512 tokens, a bound that some block reaches.
All inputs are finite; a program needn't handle non-finite values.
Results may differ from a plain program's by a relative error of at most 0.0049.
Values may be sent and summed in bfloat16 or wider, within the bound.
No kernel may reach another device: no remote copies, remote signals or barrier semaphores. Data moves between devices by JAX's collectives and lax.ppermute only.
A program may use at most 128 MiB of HBM per device.

v0:
```python
import functools

import jax
import jax.numpy as jnp
from jax import lax
from jax.experimental import pallas as pl
from jax.experimental.pallas import tpu as pltpu
from jax.sharding import PartitionSpec as P


BOTH = ("row", "col")


def place_of(i):
    row, col = divmod(i, 16)
    return col // 2 % 4, col // 8 * 2 + row % 2, row // 2, col % 2


def index_of(x, y, z, k):
    x, y, z = x % 4, y % 4, z % 4
    return (z * 2 + y % 2) * 16 + ((y // 2) * 4 + x) * 2 + k


def shifted(a, axis, by):
    pairs = []
    for i in range(128):
        x, y, z, k = place_of(i)
        if axis == "core":
            k = 1 - k
        elif axis == "z":
            z = z + by
        elif (axis == "first") == (k == 0):
            x = x + by
        else:
            y = y + by
        pairs.append((i, index_of(x, y, z, k)))
    return lax.ppermute(a.reshape(-1, 8, a.shape[-1]), BOTH, pairs)


def gathered(a, axis):
    return jnp.concatenate([a.reshape(-1, 8, a.shape[-1])] + [shifted(a, axis, -by) for by in (1, 2, 3)], axis=0)


def turn_kernel(tile_cols, inverse_ref, me_ref, x_ref, *refs):
    s_refs, (turned, staged, sems) = refs[:-3], refs[-3:]
    step = pl.program_id(0)
    local, depth, span = x_ref.shape
    half = tile_cols // 2
    tiles = s_refs[0].shape[0] // tile_cols
    lanes = 128
    same = lax.broadcasted_iota(jnp.int32, (lanes, lanes), 0) == lax.broadcasted_iota(jnp.int32, (lanes, lanes), 1)
    eye = jnp.where(same, 1.0, 0.0).astype(x_ref.dtype)

    gap = jnp.zeros((192 - depth, lanes), x_ref.dtype)
    for at in range(span // lanes):
        rows = pl.ds(pl.multiple_of(step * span + at * lanes, 8), lanes)
        part = slice(at * lanes, (at + 1) * lanes)
        stacked = jnp.concatenate([piece for e in range(local) for piece in (x_ref[e, :, part], gap)], axis=0)
        flipped = lax.dot_general(eye, stacked, (((1,), (1,)), ((), ())), preferred_element_type=jnp.float32)
        for lane in range(3):
            turned[lane, rows, :] = flipped[:, lane * lanes : (lane + 1) * lanes]

    @pl.when(step == pl.num_programs(0) - 1)
    def _():
        copies = []
        for n, s_ref in enumerate(s_refs):
            first = (me_ref[0] ^ n) * tiles
            starts = [inverse_ref[first + t] * tile_cols for t in range(tiles)]
            for lane in range(3):
                pieces = [
                    turned[lane, pl.ds(start + side, half, stride=2), :] for side in range(2) for start in starts
                ]
                whole = jnp.concatenate(pieces, axis=0).astype(staged.dtype)
                staged[n, :, lane * lanes : (lane + 1) * lanes] = whole
            copies.append(pltpu.make_async_copy(staged.at[n], s_ref, sems.at[n]))
            copies[-1].start()
        for copy in copies:
            copy.wait()


def activated(w, t, share):
    ff = w.shape[0] // 2
    pre = lax.dot_general(w, t, (((1,), (1,)), ((), ())), preferred_element_type=jnp.float32)
    gate, up = pre[:ff], pre[ff:]
    act = share * (up + 1.0) * gate * jax.nn.sigmoid(1.702 * gate)
    return act.astype(jnp.bfloat16).T


def hidden_kernel(w_ref, t_ref, share_ref, act_ref):
    for e in range(act_ref.shape[0]):
        act_ref[e] = activated(w_ref[e], t_ref[...], share_ref[e : e + 1, :])


def hidden(weights_in, tokens, share):
    local, mine, width = weights_in.shape
    rows, part = tokens.shape[0], 256
    return pl.pallas_call(
        hidden_kernel,
        grid=(rows // part,),
        in_specs=[
            pl.BlockSpec(weights_in.shape, lambda i: (0, 0, 0)),
            pl.BlockSpec((part, width), lambda i: (i, 0)),
            pl.BlockSpec((local, part), lambda i: (0, i)),
        ],
        out_specs=pl.BlockSpec((local, part, mine // 2), lambda i: (0, i, 0)),
        out_shape=jax.ShapeDtypeStruct((local, rows, mine // 2), jnp.bfloat16),
        compiler_params=pltpu.CompilerParams(vmem_limit_bytes=20 << 20),
        name="hidden",
        cost_estimate=pl.CostEstimate(flops=2 << 30, bytes_accessed=8 << 20, transcendentals=1 << 18),
    )(weights_in, tokens, share)


def projected(acts, downs):
    out = None
    for act, down in zip(acts, downs):
        term = jnp.dot(act, down, preferred_element_type=jnp.float32)
        out = term if out is None else out + term
    return out


def moved(block):
    return block % 16 * 4 + block // 16


def other_kernel(sources, me_ref, *refs):
    r_refs, (t_ref, share_ref, down_ref, w_ref, out_ref, r_in, t_in, sems) = refs[:sources], refs[sources:]
    local, _, width = down_ref.shape
    depth = width // sources
    for n, r_ref in enumerate(r_refs):
        slot = me_ref[0] ^ n
        pltpu.make_async_copy(r_ref, r_in.at[slot], sems.at[slot]).start()
    tokens_in = pltpu.make_async_copy(t_ref, t_in, sems.at[sources])
    tokens_in.start()
    for c in range(sources):
        pltpu.make_async_copy(r_refs[0], r_in.at[c], sems.at[c]).wait()
        for e in range(local):
            w_ref[e, :, c * depth : (c + 1) * depth] = r_in[c, :, e * 192 : e * 192 + depth]
    tokens_in.wait()
    acts = [activated(w_ref[e], t_in[...], share_ref[e : e + 1, :]) for e in range(local)]
    for at in range(0, width, 640):
        part = slice(at, min(at + 640, width))
        out = projected(acts, [down_ref[e, :, part] for e in range(local)])
        for block in range(out_ref.shape[0]):
            out_ref[moved(block), :, part] = out[block * 8 : (block + 1) * 8].astype(out_ref.dtype)


def emit_kernel(w_ref, gate_ref, up_ref):
    ff = gate_ref.shape[0]
    for e in range(w_ref.shape[0]):
        gate_ref[:, e, :] = w_ref[e, :ff, :]
        up_ref[:, e, :] = w_ref[e, ff:, :]


def own_kernel(act_ref, down_ref, came_ref, *out_refs):
    local, _, width = down_ref.shape
    acts = [act_ref[e] for e in range(local)]
    for at in range(0, width, 640):
        part = slice(at, min(at + 640, width))
        out = projected(acts, [down_ref[e, :, part] for e in range(local)])
        for block in range(came_ref.shape[0]):
            to = moved(block)
            both = out[block * 8 : (block + 1) * 8] + came_ref[to, :, part].astype(jnp.float32)
            ref = out_refs[to // 16]
            ref[to % 16, :, part] = both.astype(ref.dtype)


def own_call(act, down_weight, came, outs):
    vmem = pl.BlockSpec(memory_space=pltpu.VMEM)
    return pl.pallas_call(
        own_kernel,
        in_specs=[vmem] * 3,
        out_specs=[vmem] * len(outs),
        out_shape=outs,
        compiler_params=pltpu.CompilerParams(vmem_limit_bytes=20 << 20),
        name="down_own",
        cost_estimate=pl.CostEstimate(flops=1 << 30, bytes_accessed=8 << 20, transcendentals=0),
    )(act, down_weight, came)


def body(joined_weight, tile_perm, down_weight, tokens, expert_ids, route_scores):
    n_col = lax.axis_size("col")
    local, depth, width = joined_weight.shape
    tiles = tile_perm.shape[0]
    tile_cols = width // tiles
    mine = width // n_col
    ff = mine // 2
    span = 1152
    f32 = jnp.float32

    places = jnp.arange(tiles, dtype=jnp.int32)
    inverse = jnp.sum(places[:, None] * (tile_perm[:, None] == places[None, :]), axis=0)
    known = gathered(tokens, "second")
    known, inverse = lax.optimization_barrier((known, inverse))
    known = gathered(known, "first")
    me_col = lax.axis_index("col")[None]
    sent = pl.pallas_call(
        functools.partial(turn_kernel, tile_cols),
        grid_spec=pltpu.PrefetchScalarGridSpec(
            num_scalar_prefetch=2,
            grid=(width // span,),
            in_specs=[pl.BlockSpec((local, depth, span), lambda i, inv, me: (0, 0, i))],
            out_specs=[pl.BlockSpec(memory_space=pltpu.HBM)] * n_col,
            scratch_shapes=[
                pltpu.VMEM((3, width, 128), f32),
                pltpu.VMEM((n_col, mine, 384), jnp.bfloat16),
                pltpu.SemaphoreType.DMA((n_col,)),
            ],
        ),
        out_shape=[jax.ShapeDtypeStruct((mine, 384), jnp.bfloat16)] * n_col,
        compiler_params=pltpu.CompilerParams(vmem_limit_bytes=24 << 20),
        name="turn",
        cost_estimate=pl.CostEstimate(flops=4 << 30, bytes_accessed=16 << 20, transcendentals=0),
    )(inverse, me_col, joined_weight)
    known, sent = lax.optimization_barrier((known, sent))
    came = [sent[0]]
    for n in range(1, n_col):
        came.append(lax.ppermute(sent[n], "col", [(i, i ^ n) for i in range(n_col)]))
    known = gathered(known, "z")
    known_other = shifted(known, "core", 1)

    me = lax.axis_index(BOTH)
    row, col = me // 16, me % 16
    x, y, z, k = col // 2 % 4, col // 8 * 2 + row % 2, row // 2, col % 2
    at = jnp.arange(1024, dtype=jnp.int32)
    core = (k + at // 512) % 2
    first, second = at // 32 % 4, at // 8 % 4
    own_x = (x + jnp.where(core == 0, first, second)) % 4
    own_y = (y + jnp.where(core == 0, second, first)) % 4
    own_z = (z + at // 128 % 4) % 4
    owner = (own_z * 2 + own_y % 2) * 16 + (own_y // 2 * 4 + own_x) * 2 + core
    token = owner * 8 + at % 8

    expert_global = lax.axis_index("row") * local + jnp.arange(local, dtype=jnp.int32)
    weights = route_scores / jnp.sum(route_scores, axis=1, keepdims=True)
    share = jnp.sum(weights[:, :, None] * (expert_ids[:, :, None] == expert_global[None, None, :]), axis=1)
    share = jnp.take(share, token, axis=0)

    share = share.T
    known, known_other = (a.reshape(-1, a.shape[-1]) for a in (known, known_other))
    width = known.shape[1]

    def blocks(n, dtype):
        return jax.ShapeDtypeStruct((n, 8, width), dtype)

    vmem, hbm = pl.BlockSpec(memory_space=pltpu.VMEM), pl.BlockSpec(memory_space=pltpu.HBM)
    weights_in, other = pl.pallas_call(
        functools.partial(other_kernel, n_col),
        in_specs=[pl.BlockSpec(memory_space=pltpu.SMEM)] + [hbm] * (n_col + 1) + [vmem, vmem],
        out_specs=[vmem, vmem],
        out_shape=[jax.ShapeDtypeStruct((local, mine, width), jnp.bfloat16), blocks(64, jnp.bfloat16)],
        scratch_shapes=[
            pltpu.VMEM((n_col, mine, 384), jnp.bfloat16),
            pltpu.VMEM(known_other.shape, jnp.bfloat16),
            pltpu.SemaphoreType.DMA((n_col + 1,)),
        ],
        compiler_params=pltpu.CompilerParams(vmem_limit_bytes=32 << 20),
        name="other",
        cost_estimate=pl.CostEstimate(flops=4 << 30, bytes_accessed=16 << 20, transcendentals=1 << 18),
    )(me_col, *came, known_other, share[:, 512:], down_weight)
    came_over = shifted(other, "core", 1)
    act = hidden(weights_in, known, share[:, :512])
    outs = [blocks(16, f32)] + [blocks(16, jnp.bfloat16)] * 3
    total, *parts = own_call(act, down_weight, came_over, outs)
    weights_in, total = lax.optimization_barrier((weights_in, total))
    unit_major = jax.ShapeDtypeStruct((ff, local, width), jnp.bfloat16)
    gate_out, up_out = (
        a.transpose(1, 2, 0)
        for a in pl.pallas_call(
            emit_kernel,
            out_shape=[unit_major, unit_major],
            compiler_params=pltpu.CompilerParams(vmem_limit_bytes=20 << 20),
            name="emit",
            cost_estimate=pl.CostEstimate(flops=2 << 30, bytes_accessed=8 << 20, transcendentals=0),
        )(weights_in)
    )
    parts = [shifted(parts[by - 1], "first", by).astype(f32) for by in (1, 2, 3)]
    total = total + parts[0] + parts[1] + parts[2]
    total, gate_out, up_out = lax.optimization_barrier((total, gate_out, up_out))
    for axis, sent_as in (("second", jnp.bfloat16), ("z", f32)):
        total = total.reshape(4, -1, 8, width)
        parts = [shifted(total[by].astype(sent_as), axis, by).astype(f32) for by in (1, 2, 3)]
        total = total[0] + parts[0] + parts[1] + parts[2]
    total = total.reshape(8, width)
    return (gate_out, up_out, total.astype(jnp.bfloat16))


def solution(mesh):
    placed = (P("row", "col", None), P(), P("row", "col", None), P(("row", "col"), None), P(), P())
    return jax.shard_map(
        body,
        mesh=mesh,
        in_specs=placed,
        out_specs=(P("row", None, "col"), P("row", None, "col"), P(("row", "col"), None)),
        check_vma=False,
    )
```

profile of v0, /device:TPU:0, one launch (start us, length us, event | category | flops | bytes accessed | tf_op | source)
XLA Modules:
  0.0 200.1 jit_solution(11736264868701889350)
XLA Ops:
  0.6 1.8 collective-permute-start.2
  2.4 2.9 %collective-permute-start.1 = (bf16[1,8,2880]{2,1,0:T(8,128)(2,1)}, bf16[1,8,2880]{2,1,0:T(8,128)(2,1)S(1)}, u32[]{:S(2)}, u32[]{:S(2)}) collective-permute-start(bf16[1,8,2880]{2,1,0:T(8,128)(2,1)} %bitcast.13), channel_id=1, source_target_pairs={{0,8},{1,5},{2,10},{3,7},{4,12},{5,1},{6,14},{7,3},{8,0},{9,13},{1... | collective-permute-start | bytes 138248 | tf_op jit(solution)/shard_map/ppermute | solution.py:37
  5.3 1.3 collective-permute-start
  6.6 0.8 select_reduce_fusion.inverse_ref
  7.4 2.6 %copy.21.x_ref = bf16[2,180,5760]{2,1,0:T(8,128)(2,1)S(1)} copy(bf16[2,180,5760]{2,0,1:T(2,128)(2,1)} %param.6) | data formatting | bytes 8294400 | tf_op args[0]
  10.1 1.6 collective-permute-start.5
  11.7 2.7 %collective-permute-start.4 = (bf16[4,8,2880]{2,1,0:T(8,128)(2,1)S(1)}, bf16[4,8,2880]{2,1,0:T(8,128)(2,1)S(1)}, u32[]{:S(2)}, u32[]{:S(2)}) collective-permute-start(bf16[4,8,2880]{2,1,0:T(8,128)(2,1)S(1)} %pad_maximum_fusion.1), channel_id=1, source_target_pairs={{0,4},{1,9},{2,6},{3,11},{4,0},{5,13},{6,2},{7,15},{8,12},{9,1},{1... | collective-permute-start | bytes 552968 | tf_op jit(solution)/shard_map/ppermute | solution.py:37
  14.4 1.4 collective-permute-start.3
  15.9 5.4 %turn.1 = (bf16[360,384]{1,0:T(8,128)(2,1)S(1)}, bf16[360,384]{1,0:T(8,128)(2,1)}, bf16[360,384]{1,0:T(8,128)(2,1)}, bf16[360,384]{1,0:T(8,128)(2,1)}, bf16[360,...) custom-call(s32[144]{0:T(256)S(1)} %select_reduce_fusion.inverse_ref, ...), custom_call_target="tpu_custom_call" | custom-call | flops 4294967296 | bytes 16777216 | tf_op jit(solution)/shard_map/turn/pallas_call | solution.py:196
  21.2 0.7 copy-done.5
  21.9 0.7 copy-done.6
  22.6 0.7 copy-done.7
  23.3 0.7 copy-done.8
  24.0 0.7 copy-done.9
  24.8 0.7 copy-done.10
  25.5 0.7 copy-done.11
  26.4 4.1 %collective-permute-start.21 = (bf16[16,8,2880]{2,1,0:T(8,128)(2,1)S(1)}, bf16[16,8,2880]{2,1,0:T(8,128)(2,1)S(1)}, u32[]{:S(2)}, u32[]{:S(2)}) collective-permute-start(bf16[16,8,2880]{2,1,0:T(8,128)(2,1)S(1)} %pad_maximum_fusion), channel_id=1, source_target_pairs={{0,96},{1,97},{2,98},{3,99},{4,100},{5,101},{6,102},{7,103},{8,104... | collective-permute-start | bytes 2211848 | tf_op jit(solution)/shard_map/ppermute | solution.py:37
  30.5 1.3 collective-permute-start.23
  31.8 29.2 %collective-permute-done.21 = bf16[16,8,2880]{2,1,0:T(8,128)(2,1)S(1)} collective-permute-done((bf16[16,8,2880]{2,1,0:T(8,128)(2,1)S(1)}, bf16[16,8,2880]{2,1,0:T(8,128)(2,1)S(1)}, u32[]{:S(2)}, u32[]{:S(2)}) %collective-permute-start.21) | collective-permute-done | bytes 737312 | tf_op jit(solution)/shard_map/ppermute | solution.py:37
  61.3 3.2 %collective-permute-done.23 = bf16[16,8,2880]{2,1,0:T(8,128)(2,1)S(1)} collective-permute-done((bf16[16,8,2880]{2,1,0:T(8,128)(2,1)S(1)}, bf16[16,8,2880]{2,1,0:T(8,128)(2,1)S(1)}, u32[]{:S(2)}, u32[]{:S(2)}) %collective-permute-start.23) | collective-permute-done | bytes 737312 | tf_op jit(solution)/shard_map/ppermute | solution.py:37
  64.7 0.5 collective-permute-start.6
  65.2 0.6 collective-permute-start.7
  65.8 0.9 collective-permute-start.8
  66.7 1.3 collective-permute-start.9
  67.9 2.7 %collective-permute-done.6.refs_1_ = bf16[360,384]{1,0:T(8,128)(2,1)} collective-permute-done((bf16[360,384]{1,0:T(8,128)(2,1)}, bf16[360,384]{1,0:T(8,128)(2,1)}, u32[]{:S(2)}, u32[]{:S(2)}) %collective-permute-start.6) | collective-permute-done | bytes 276512 | tf_op jit(solution)/shard_map/ppermute | solution.py:217
  70.9 4.1 %collective-permute-done.7.refs_2_ = bf16[360,384]{1,0:T(8,128)(2,1)} collective-permute-done((bf16[360,384]{1,0:T(8,128)(2,1)}, bf16[360,384]{1,0:T(8,128)(2,1)}, u32[]{:S(2)}, u32[]{:S(2)}) %collective-permute-start.7) | collective-permute-done | bytes 276512 | tf_op jit(solution)/shard_map/ppermute | solution.py:217
  75.0 1.2 collective-permute-start.11
  76.1 3.0 %collective-permute-done.8.refs_3_ = bf16[360,384]{1,0:T(8,128)(2,1)} collective-permute-done((bf16[360,384]{1,0:T(8,128)(2,1)}, bf16[360,384]{1,0:T(8,128)(2,1)}, u32[]{:S(2)}, u32[]{:S(2)}) %collective-permute-start.8) | collective-permute-done | bytes 276512 | tf_op jit(solution)/shard_map/ppermute | solution.py:217
  79.1 2.6 %collective-permute-start.12 = (bf16[360,384]{1,0:T(8,128)(2,1)}, bf16[360,384]{1,0:T(8,128)(2,1)}, u32[]{:S(2)}, u32[]{:S(2)}) collective-permute-start(bf16[360,384]{1,0:T(8,128)(2,1)} %copy-done.7), channel_id=1, source_target_pairs={{0,7},{1,6},{2,5},{3,4},{4,3},{5,2},{6,1},{7,0},{8,15},{9,14},{10,... | collective-permute-start | bytes 829448 | tf_op jit(solution)/shard_map/ppermute | solution.py:217
  81.9 1.0 copy.22
  83.0 4.5 %collective-permute-done.9.refs_4_ = bf16[360,384]{1,0:T(8,128)(2,1)} collective-permute-done((bf16[360,384]{1,0:T(8,128)(2,1)}, bf16[360,384]{1,0:T(8,128)(2,1)}, u32[]{:S(2)}, u32[]{:S(2)}) %collective-permute-start.9) | collective-permute-done | bytes 276512 | tf_op jit(solution)/shard_map/ppermute | solution.py:217
  88.0 3.7 %collective-permute-done.10.refs_5_ = bf16[360,384]{1,0:T(8,128)(2,1)} collective-permute-done((bf16[360,384]{1,0:T(8,128)(2,1)}, bf16[360,384]{1,0:T(8,128)(2,1)}, u32[]{:S(2)}, u32[]{:S(2)}) %collective-permute-start.10) | collective-permute-done | bytes 276512 | tf_op jit(solution)/shard_map/ppermute | solution.py:217
  91.7 0.8 collective-permute-start.14
  92.5 5.2 %collective-permute-done.11.refs_6_ = bf16[360,384]{1,0:T(8,128)(2,1)} collective-permute-done((bf16[360,384]{1,0:T(8,128)(2,1)}, bf16[360,384]{1,0:T(8,128)(2,1)}, u32[]{:S(2)}, u32[]{:S(2)}) %collective-permute-start.11) | collective-permute-done | bytes 276512 | tf_op jit(solution)/shard_map/ppermute | solution.py:217
  97.7 1.0 collective-permute-done.12.refs_7_
  98.7 1.5 collective-permute-start.16
  100.2 5.1 %gather_fusion = f32[1024,2]{1,0:T(8,128)} fusion(f32[1024,2]{1,0:T(8,128)} %copy.22, s32[1024]{0:T(1024)S(1)} %broadcast_clamp_fusion), kind=kCustom, calls=%fused_computation | custom fusion | bytes 20480 | tf_op jit(solution)/shard_map/jit(_take)/gather | solution.py:236
  105.3 1.2 copy.23
  106.5 5.8 %collective-permute-start.17 = (bf16[360,384]{1,0:T(8,128)(2,1)}, bf16[360,384]{1,0:T(8,128)(2,1)S(1)}, u32[]{:S(2)}, u32[]{:S(2)}) collective-permute-start(bf16[360,384]{1,0:T(8,128)(2,1)} %copy-done.2), channel_id=1, source_target_pairs={{0,12},{1,13},{2,14},{3,15},{4,8},{5,9},{6,10},{7,11},{8,4},{9,5},... | collective-permute-start | bytes 829448 | tf_op jit(solution)/shard_map/ppermute | solution.py:217
  112.3 1.1 collective-permute-done.14.refs_9_
  113.4 1.8 collective-permute-start.18
  115.2 6.1 %collective-permute-start.19 = (bf16[360,384]{1,0:T(8,128)(2,1)}, bf16[360,384]{1,0:T(8,128)(2,1)S(1)}, u32[]{:S(2)}, u32[]{:S(2)}) collective-permute-start(bf16[360,384]{1,0:T(8,128)(2,1)} %copy-done), channel_id=1, source_target_pairs={{0,14},{1,15},{2,12},{3,13},{4,10},{5,11},{6,8},{7,9},{8,6},{9,7},... | collective-permute-start | bytes 829448 | tf_op jit(solution)/shard_map/ppermute | solution.py:217
  121.3 4.5 %collective-permute-start.20 = (bf16[360,384]{1,0:T(8,128)(2,1)S(1)}, bf16[360,384]{1,0:T(8,128)(2,1)S(1)}, u32[]{:S(2)}, u32[]{:S(2)}) collective-permute-start(bf16[360,384]{1,0:T(8,128)(2,1)S(1)} %get-tuple-element.84), channel_id=1, source_target_pairs={{0,15},{1,14},{2,13},{3,12},{4,11},{5,10},{6,9},{7,8},{8,7},{9,6},... | collective-permute-start | bytes 829448 | tf_op jit(solution)/shard_map/ppermute | solution.py:217
  125.8 1.8 copy.24.refs_18_.down_ref
  127.7 3.9 %collective-permute-done.19.refs_14_ = bf16[360,384]{1,0:T(8,128)(2,1)S(1)} collective-permute-done((bf16[360,384]{1,0:T(8,128)(2,1)}, bf16[360,384]{1,0:T(8,128)(2,1)S(1)}, u32[]{:S(2)}, u32[]{:S(2)}) %collective-permute-start.19) | collective-permute-done | bytes 276512 | tf_op jit(solution)/shard_map/ppermute | solution.py:217
  131.5 6.7 %collective-permute-done.20.refs_15_ = bf16[360,384]{1,0:T(8,128)(2,1)S(1)} collective-permute-done((bf16[360,384]{1,0:T(8,128)(2,1)S(1)}, bf16[360,384]{1,0:T(8,128)(2,1)S(1)}, u32[]{:S(2)}, u32[]{:S(2)}) %collective-permute-start.20) | collective-permute-done | bytes 276512 | tf_op jit(solution)/shard_map/ppermute | solution.py:217
  138.3 8.3 %other.1 = (bf16[2,360,2880]{2,1,0:T(8,128)(2,1)S(1)}, bf16[64,8,2880]{2,1,0:T(8,128)(2,1)S(1)}) custom-call(s32[1]{0:T(128)} %bitcast.me_ref, bf16[360,384]{1,0:T(8,128)(2,1)S(1)} %copy-done.12, bf16[360,384]{1,0:T(8,128)(2,1)} %collective-permute-done.6.refs_1_, bf16[360,384]{1,0:T(8,128)(2,1)} %collective-permute-done.7.refs_2_, ...), custom_call_target="tpu_custom_call" | custom-call | flops 4294967296 | bytes 16777216 | tf_op jit(solution)/shard_map/other/pallas_call | solution.py:246
  146.7 3.2 %hidden.1.act_ref = bf16[2,512,180]{2,1,0:T(8,128)(2,1)S(1)} custom-call(bf16[2,360,2880]{2,1,0:T(8,128)(2,1)S(1)} %get-tuple-element.93.w_ref, bf16[512,2880]{1,0:T(8,128)(2,1)S(1)} %bitcast.11, f32[2,512]{1,0:T(2,128)S(1)} %get-tuple-element.105.share_ref), custom_call_target="tpu_custom_call" | custom-call | flops 2147483648 | bytes 8388608 | tf_op jit(solution)/shard_map/hidden/pallas_call | solution.py:97
  149.9 2.3 %collective-permute-done.25.came_ref = bf16[64,8,2880]{2,1,0:T(8,128)(2,1)S(1)} collective-permute-done((bf16[64,8,2880]{2,1,0:T(8,128)(2,1)S(1)}, bf16[64,8,2880]{2,1,0:T(8,128)(2,1)S(1)}, u32[]{:S(2)}, u32[]{:S(2)}) %collective-permute-start.25) | collective-permute-done | bytes 2949152 | tf_op jit(solution)/shard_map/ppermute | solution.py:37
  152.2 2.1 %down_own.1 = (f32[16,8,2880]{2,1,0:T(8,128)S(1)}, bf16[16,8,2880]{2,1,0:T(8,128)(2,1)S(1)}, bf16[16,8,2880]{2,1,0:T(8,128)(2,1)S(1)}, bf16[16,8,2880]{2,1,0:T(8,128)(2,1)S(1)}) custom-call(bf16[2,512,180]{2,1,0:T(8,128)(2,1)S(1)} %hidden.1.act_ref, bf16[2,180,2880]{2,1,0:T(8,128)(2,1)S(1)} %copy.24.refs_18_.down_ref, ...), custom_call_target="tpu_custom_call" | custom-call | flops 1073741824 | bytes 8388608 | tf_op jit(solution)/shard_map/down_own/pallas_call | solution.py:169
  154.2 0.5 collective-permute-start.26
  154.8 6.6 %collective-permute-start.27 = (bf16[16,8,2880]{2,1,0:T(8,128)(2,1)S(1)}, bf16[16,8,2880]{2,1,0:T(8,128)(2,1)S(1)}, u32[]{:S(2)}, u32[]{:S(2)}) collective-permute-start(bf16[16,8,2880]{2,1,0:T(8,128)(2,1)S(1)} %get-tuple-element.91), channel_id=1, source_target_pairs={{0,4},{1,9},{2,6},{3,11},{4,0},{5,13},{6,2},{7,15},{8,12},{9,1},{1... | collective-permute-start | bytes 2211848 | tf_op jit(solution)/shard_map/ppermute | solution.py:37
  161.4 3.7 %emit.1 = (bf16[180,2,2880]{2,1,0:T(2,128)(2,1)}, bf16[180,2,2880]{2,1,0:T(2,128)(2,1)}) custom-call(bf16[2,360,2880]{2,1,0:T(8,128)(2,1)S(1)} %get-tuple-element.93.w_ref), custom_call_target="tpu_custom_call" | custom-call | flops 2147483648 | bytes 8388608 | tf_op jit(solution)/shard_map/emit/pallas_call | solution.py:268
  165.1 4.4 %collective-permute-done.26 = bf16[16,8,2880]{2,1,0:T(8,128)(2,1)S(1)} collective-permute-done((bf16[16,8,2880]{2,1,0:T(8,128)(2,1)S(1)}, bf16[16,8,2880]{2,1,0:T(8,128)(2,1)S(1)}, u32[]{:S(2)}, u32[]{:S(2)}) %collective-permute-start.26) | collective-permute-done | bytes 737312 | tf_op jit(solution)/shard_map/ppermute | solution.py:37
  169.5 9.5 %collective-permute-done.27 = bf16[16,8,2880]{2,1,0:T(8,128)(2,1)S(1)} collective-permute-done((bf16[16,8,2880]{2,1,0:T(8,128)(2,1)S(1)}, bf16[16,8,2880]{2,1,0:T(8,128)(2,1)S(1)}, u32[]{:S(2)}, u32[]{:S(2)}) %collective-permute-start.27) | collective-permute-done | bytes 737312 | tf_op jit(solution)/shard_map/ppermute | solution.py:37
  179.5 0.7 collective-permute-start.29
  180.2 2.6 %collective-permute-start.31 = (bf16[4,8,2880]{2,1,0:T(8,128)(2,1)S(1)}, bf16[4,8,2880]{2,1,0:T(8,128)(2,1)S(1)}, u32[]{:S(2)}, u32[]{:S(2)}) collective-permute-start(bf16[4,8,2880]{2,1,0:T(8,128)(2,1)S(1)} %get-tuple-element.100), channel_id=1, source_target_pairs={{0,24},{1,7},{2,26},{3,1},{4,28},{5,3},{6,30},{7,5},{8,16},{9,15},... | collective-permute-start | bytes 552968 | tf_op jit(solution)/shard_map/ppermute | solution.py:37
  182.8 3.6 %collective-permute-done.29 = bf16[4,8,2880]{2,1,0:T(8,128)(2,1)S(1)} collective-permute-done((bf16[4,8,2880]{2,1,0:T(8,128)(2,1)S(1)}, bf16[4,8,2880]{2,1,0:T(8,128)(2,1)S(1)}, u32[]{:S(2)}, u32[]{:S(2)}) %collective-permute-start.29) | collective-permute-done | bytes 184352 | tf_op jit(solution)/shard_map/ppermute | solution.py:37
  186.4 1.6 collective-permute-done.31
  188.0 1.9 collective-permute-done.30
  190.1 3.2 %collective-permute-start.34 = (f32[1,8,2880]{2,1,0:T(8,128)S(1)}, f32[1,8,2880]{2,1,0:T(8,128)S(1)}, u32[]{:S(2)}, u32[]{:S(2)}) collective-permute-start(f32[1,8,2880]{2,1,0:T(8,128)S(1)} %get-tuple-element.103), channel_id=1, source_target_pairs={{0,96},{1,97},{2,98},{3,99},{4,100},{5,101},{6,102},{7,103},{8,104... | collective-permute-start | bytes 276488 | tf_op jit(solution)/shard_map/ppermute | solution.py:37
  193.3 3.2 %collective-permute-done.32 = f32[1,8,2880]{2,1,0:T(8,128)S(1)} collective-permute-done((f32[1,8,2880]{2,1,0:T(8,128)S(1)}, f32[1,8,2880]{2,1,0:T(8,128)S(1)}, u32[]{:S(2)}, u32[]{:S(2)}) %collective-permute-start.32) | collective-permute-done | bytes 92192 | tf_op jit(solution)/shard_map/ppermute | solution.py:37
  196.5 2.9 %collective-permute-done.33 = f32[1,8,2880]{2,1,0:T(8,128)S(1)} collective-permute-done((f32[1,8,2880]{2,1,0:T(8,128)S(1)}, f32[1,8,2880]{2,1,0:T(8,128)S(1)}, u32[]{:S(2)}, u32[]{:S(2)}) %collective-permute-start.33) | collective-permute-done | bytes 92192 | tf_op jit(solution)/shard_map/ppermute | solution.py:37
  199.4 0.7 fusion.3
  (70 shorter events, 2.4 us)
Async XLA Ops:
  0.6 9.4 %collective-permute-start.2 = (bf16[1,8,2880]{2,1,0:T(8,128)(2,1)}, bf16[1,8,2880]{2,1,0:T(8,128)(2,1)S(1)}, u32[]{:S(2)}, u32[]{:S(2)}) collective-permute-start(bf16[1,8,2880]{2,1,0:T(8,128)(2,1)} %bitcast.12), channel_id=1, source_target_pairs={{0,16},{1,3},{2,18},{3,5},{4,20},{5,7},{6,22},{7,1},{8,24},{9,11},... | collective-permute-start | bytes 138248 | tf_op jit(solution)/shard_map/ppermute | solution.py:37
  2.4 7.7 %collective-permute-start.1 = (bf16[1,8,2880]{2,1,0:T(8,128)(2,1)}, bf16[1,8,2880]{2,1,0:T(8,128)(2,1)S(1)}, u32[]{:S(2)}, u32[]{:S(2)}) collective-permute-start(bf16[1,8,2880]{2,1,0:T(8,128)(2,1)} %bitcast.13), channel_id=1, source_target_pairs={{0,8},{1,5},{2,10},{3,7},{4,12},{5,1},{6,14},{7,3},{8,0},{9,13},{1... | collective-permute-start | bytes 138248 | tf_op jit(solution)/shard_map/ppermute | solution.py:37
  5.3 4.8 %collective-permute-start = (bf16[1,8,2880]{2,1,0:T(8,128)(2,1)}, bf16[1,8,2880]{2,1,0:T(8,128)(2,1)S(1)}, u32[]{:S(2)}, u32[]{:S(2)}) collective-permute-start(bf16[1,8,2880]{2,1,0:T(8,128)(2,1)} %bitcast.14), channel_id=1, source_target_pairs={{0,24},{1,7},{2,26},{3,1},{4,28},{5,3},{6,30},{7,5},{8,16},{9,15},... | collective-permute-start | bytes 138248 | tf_op jit(solution)/shard_map/ppermute | solution.py:37
  7.4 2.7 %copy-start.14 = (bf16[8,2880]{1,0:T(8,128)(2,1)S(1)}, bf16[8,2880]{1,0:T(8,128)(2,1)}, u32[]{:S(2)}) copy-start(bf16[8,2880]{1,0:T(8,128)(2,1)} %param.9) | copy-start | bytes 138244
  10.1 16.1 %collective-permute-start.5 = (bf16[4,8,2880]{2,1,0:T(8,128)(2,1)S(1)}, bf16[4,8,2880]{2,1,0:T(8,128)(2,1)S(1)}, u32[]{:S(2)}, u32[]{:S(2)}) collective-permute-start(bf16[4,8,2880]{2,1,0:T(8,128)(2,1)S(1)} %pad_maximum_fusion.1), channel_id=1, source_target_pairs={{0,2},{1,17},{2,4},{3,19},{4,6},{5,21},{6,0},{7,23},{8,10},{9,25},... | collective-permute-start | bytes 552968 | tf_op jit(solution)/shard_map/ppermute | solution.py:37
  11.7 14.5 %collective-permute-start.4 = (bf16[4,8,2880]{2,1,0:T(8,128)(2,1)S(1)}, bf16[4,8,2880]{2,1,0:T(8,128)(2,1)S(1)}, u32[]{:S(2)}, u32[]{:S(2)}) collective-permute-start(bf16[4,8,2880]{2,1,0:T(8,128)(2,1)S(1)} %pad_maximum_fusion.1), channel_id=1, source_target_pairs={{0,4},{1,9},{2,6},{3,11},{4,0},{5,13},{6,2},{7,15},{8,12},{9,1},{1... | collective-permute-start | bytes 552968 | tf_op jit(solution)/shard_map/ppermute | solution.py:37
  14.4 11.8 %collective-permute-start.3 = (bf16[4,8,2880]{2,1,0:T(8,128)(2,1)S(1)}, bf16[4,8,2880]{2,1,0:T(8,128)(2,1)S(1)}, u32[]{:S(2)}, u32[]{:S(2)}) collective-permute-start(bf16[4,8,2880]{2,1,0:T(8,128)(2,1)S(1)} %pad_maximum_fusion.1), channel_id=1, source_target_pairs={{0,6},{1,25},{2,0},{3,27},{4,2},{5,29},{6,4},{7,31},{8,14},{9,17},... | collective-permute-start | bytes 552968 | tf_op jit(solution)/shard_map/ppermute | solution.py:37
  21.2 0.7 copy-start.5
  21.9 0.7 copy-start.6
  22.6 0.7 copy-start.7
  23.3 0.7 copy-start.8
  24.0 0.7 copy-start.9
  24.8 0.7 copy-start.10
  25.5 0.7 copy-start.11
  26.2 35.1 %copy-start = (bf16[360,384]{1,0:T(8,128)(2,1)}, bf16[360,384]{1,0:T(8,128)(2,1)S(1)}, u32[]{:S(2)}) copy-start(bf16[360,384]{1,0:T(8,128)(2,1)S(1)} %get-tuple-element.83) | copy-start | bytes 829444
  26.2 35.1 %copy-start.1 = (bf16[360,384]{1,0:T(8,128)(2,1)}, bf16[360,384]{1,0:T(8,128)(2,1)S(1)}, u32[]{:S(2)}) copy-start(bf16[360,384]{1,0:T(8,128)(2,1)S(1)} %get-tuple-element.82) | copy-start | bytes 829444
  26.2 35.1 %copy-start.2 = (bf16[360,384]{1,0:T(8,128)(2,1)}, bf16[360,384]{1,0:T(8,128)(2,1)S(1)}, u32[]{:S(2)}) copy-start(bf16[360,384]{1,0:T(8,128)(2,1)S(1)} %get-tuple-element.81) | copy-start | bytes 829444
  26.2 35.1 %copy-start.3 = (bf16[360,384]{1,0:T(8,128)(2,1)}, bf16[360,384]{1,0:T(8,128)(2,1)S(1)}, u32[]{:S(2)}) copy-start(bf16[360,384]{1,0:T(8,128)(2,1)S(1)} %get-tuple-element.80) | copy-start | bytes 829444
  26.2 35.1 %copy-start.4 = (bf16[360,384]{1,0:T(8,128)(2,1)}, bf16[360,384]{1,0:T(8,128)(2,1)S(1)}, u32[]{:S(2)}) copy-start(bf16[360,384]{1,0:T(8,128)(2,1)S(1)} %get-tuple-element.79) | copy-start | bytes 829444
  26.4 40.2 %copy-start.13 = (f32[1024,4]{0,1:T(4,128)S(1)}, f32[1024,4]{0,1:T(4,128)}, u32[]{:S(2)}) copy-start(f32[1024,4]{0,1:T(4,128)} %param.11) | copy-start | bytes 49156
  26.4 55.4 %copy-start.15 = (s32[1024,4]{0,1:T(4,128)S(1)}, s32[1024,4]{0,1:T(4,128)}, u32[]{:S(2)}) copy-start(s32[1024,4]{0,1:T(4,128)} %param.10) | copy-start | bytes 49156
  26.4 34.7 %collective-permute-start.21 = (bf16[16,8,2880]{2,1,0:T(8,128)(2,1)S(1)}, bf16[16,8,2880]{2,1,0:T(8,128)(2,1)S(1)}, u32[]{:S(2)}, u32[]{:S(2)}) collective-permute-start(bf16[16,8,2880]{2,1,0:T(8,128)(2,1)S(1)} %pad_maximum_fusion), channel_id=1, source_target_pairs={{0,96},{1,97},{2,98},{3,99},{4,100},{5,101},{6,102},{7,103},{8,104... | collective-permute-start | bytes 2211848 | tf_op jit(solution)/shard_map/ppermute | solution.py:37
  30.5 30.7 %collective-permute-start.22 = (bf16[16,8,2880]{2,1,0:T(8,128)(2,1)S(1)}, bf16[16,8,2880]{2,1,0:T(8,128)(2,1)S(1)}, u32[]{:S(2)}, u32[]{:S(2)}) collective-permute-start(bf16[16,8,2880]{2,1,0:T(8,128)(2,1)S(1)} %pad_maximum_fusion), channel_id=1, source_target_pairs={{0,64},{1,65},{2,66},{3,67},{4,68},{5,69},{6,70},{7,71},{8,72},{9,... | collective-permute-start | bytes 2211848 | tf_op jit(solution)/shard_map/ppermute | solution.py:37
  30.5 34.0 %collective-permute-start.23 = (bf16[16,8,2880]{2,1,0:T(8,128)(2,1)S(1)}, bf16[16,8,2880]{2,1,0:T(8,128)(2,1)S(1)}, u32[]{:S(2)}, u32[]{:S(2)}) collective-permute-start(bf16[16,8,2880]{2,1,0:T(8,128)(2,1)S(1)} %pad_maximum_fusion), channel_id=1, source_target_pairs={{0,32},{1,33},{2,34},{3,35},{4,36},{5,37},{6,38},{7,39},{8,40},{9,... | collective-permute-start | bytes 2211848 | tf_op jit(solution)/shard_map/ppermute | solution.py:37
  64.6 73.7 %collective-permute-start.24 = (bf16[64,8,2880]{2,1,0:T(8,128)(2,1)S(1)}, bf16[64,8,2880]{2,1,0:T(8,128)(2,1)}, u32[]{:S(2)}, u32[]{:S(2)}) collective-permute-start(bf16[64,8,2880]{2,1,0:T(8,128)(2,1)S(1)} %constant_dynamic-update-slice_fusion), channel_id=1, source_target_pairs={{0,1},{1,0},{2,3},{3,2},{4,5},{5,4},{6,7},{7,6},{8,9},{9,8},{10,11... | collective-permute-start | bytes 8847368 | tf_op jit(solution)/shard_map/ppermute | solution.py:37
  64.7 6.0 %collective-permute-start.6 = (bf16[360,384]{1,0:T(8,128)(2,1)}, bf16[360,384]{1,0:T(8,128)(2,1)}, u32[]{:S(2)}, u32[]{:S(2)}) collective-permute-start(bf16[360,384]{1,0:T(8,128)(2,1)} %get-tuple-element.70), channel_id=1, source_target_pairs={{0,1},{1,0},{2,3},{3,2},{4,5},{5,4},{6,7},{7,6},{8,9},{9,8},{10,11... | collective-permute-start | bytes 829448 | tf_op jit(solution)/shard_map/ppermute | solution.py:217
  65.2 9.8 %collective-permute-start.7 = (bf16[360,384]{1,0:T(8,128)(2,1)}, bf16[360,384]{1,0:T(8,128)(2,1)}, u32[]{:S(2)}, u32[]{:S(2)}) collective-permute-start(bf16[360,384]{1,0:T(8,128)(2,1)} %get-tuple-element.71), channel_id=1, source_target_pairs={{0,2},{1,3},{2,0},{3,1},{4,6},{5,7},{6,4},{7,5},{8,10},{9,11},{10,... | collective-permute-start | bytes 829448 | tf_op jit(solution)/shard_map/ppermute | solution.py:217
  65.8 13.4 %collective-permute-start.8 = (bf16[360,384]{1,0:T(8,128)(2,1)}, bf16[360,384]{1,0:T(8,128)(2,1)}, u32[]{:S(2)}, u32[]{:S(2)}) collective-permute-start(bf16[360,384]{1,0:T(8,128)(2,1)} %get-tuple-element.72), channel_id=1, source_target_pairs={{0,3},{1,2},{2,1},{3,0},{4,7},{5,6},{6,5},{7,4},{8,11},{9,10},{10,... | collective-permute-start | bytes 829448 | tf_op jit(solution)/shard_map/ppermute | solution.py:217
  66.7 20.9 %collective-permute-start.9 = (bf16[360,384]{1,0:T(8,128)(2,1)}, bf16[360,384]{1,0:T(8,128)(2,1)}, u32[]{:S(2)}, u32[]{:S(2)}) collective-permute-start(bf16[360,384]{1,0:T(8,128)(2,1)} %copy-done.10), channel_id=1, source_target_pairs={{0,4},{1,5},{2,6},{3,7},{4,0},{5,1},{6,2},{7,3},{8,12},{9,13},{10,... | collective-permute-start | bytes 829448 | tf_op jit(solution)/shard_map/ppermute | solution.py:217
  70.7 21.0 %collective-permute-start.10 = (bf16[360,384]{1,0:T(8,128)(2,1)}, bf16[360,384]{1,0:T(8,128)(2,1)}, u32[]{:S(2)}, u32[]{:S(2)}) collective-permute-start(bf16[360,384]{1,0:T(8,128)(2,1)} %copy-done.9), channel_id=1, source_target_pairs={{0,5},{1,4},{2,7},{3,6},{4,1},{5,0},{6,3},{7,2},{8,13},{9,12},{10,... | collective-permute-start | bytes 829448 | tf_op jit(solution)/shard_map/ppermute | solution.py:217
  75.0 22.7 %collective-permute-start.11 = (bf16[360,384]{1,0:T(8,128)(2,1)}, bf16[360,384]{1,0:T(8,128)(2,1)}, u32[]{:S(2)}, u32[]{:S(2)}) collective-permute-start(bf16[360,384]{1,0:T(8,128)(2,1)} %copy-done.8), channel_id=1, source_target_pairs={{0,6},{1,7},{2,4},{3,5},{4,2},{5,3},{6,0},{7,1},{8,14},{9,15},{10,... | collective-permute-start | bytes 829448 | tf_op jit(solution)/shard_map/ppermute | solution.py:217
  79.1 19.6 %collective-permute-start.12 = (bf16[360,384]{1,0:T(8,128)(2,1)}, bf16[360,384]{1,0:T(8,128)(2,1)}, u32[]{:S(2)}, u32[]{:S(2)}) collective-permute-start(bf16[360,384]{1,0:T(8,128)(2,1)} %copy-done.7), channel_id=1, source_target_pairs={{0,7},{1,6},{2,5},{3,4},{4,3},{5,2},{6,1},{7,0},{8,15},{9,14},{10,... | collective-permute-start | bytes 829448 | tf_op jit(solution)/shard_map/ppermute | solution.py:217
  87.5 19.0 %collective-permute-start.13 = (bf16[360,384]{1,0:T(8,128)(2,1)}, bf16[360,384]{1,0:T(8,128)(2,1)}, u32[]{:S(2)}, u32[]{:S(2)}) collective-permute-start(bf16[360,384]{1,0:T(8,128)(2,1)} %copy-done.6), channel_id=1, source_target_pairs={{0,8},{1,9},{2,10},{3,11},{4,12},{5,13},{6,14},{7,15},{8,0},{9,1},... | collective-permute-start | bytes 829448 | tf_op jit(solution)/shard_map/ppermute | solution.py:217
  91.7 21.7 %collective-permute-start.14 = (bf16[360,384]{1,0:T(8,128)(2,1)}, bf16[360,384]{1,0:T(8,128)(2,1)}, u32[]{:S(2)}, u32[]{:S(2)}) collective-permute-start(bf16[360,384]{1,0:T(8,128)(2,1)} %copy-done.5), channel_id=1, source_target_pairs={{0,9},{1,8},{2,11},{3,10},{4,13},{5,12},{6,15},{7,14},{8,1},{9,0},... | collective-permute-start | bytes 829448 | tf_op jit(solution)/shard_map/ppermute | solution.py:217
  97.7 17.5 %collective-permute-start.15 = (bf16[360,384]{1,0:T(8,128)(2,1)}, bf16[360,384]{1,0:T(8,128)(2,1)}, u32[]{:S(2)}, u32[]{:S(2)}) collective-permute-start(bf16[360,384]{1,0:T(8,128)(2,1)} %copy-done.4), channel_id=1, source_target_pairs={{0,10},{1,11},{2,8},{3,9},{4,14},{5,15},{6,12},{7,13},{8,2},{9,3},... | collective-permute-start | bytes 829448 | tf_op jit(solution)/shard_map/ppermute | solution.py:217
  98.7 22.6 %collective-permute-start.16 = (bf16[360,384]{1,0:T(8,128)(2,1)}, bf16[360,384]{1,0:T(8,128)(2,1)}, u32[]{:S(2)}, u32[]{:S(2)}) collective-permute-start(bf16[360,384]{1,0:T(8,128)(2,1)} %copy-done.3), channel_id=1, source_target_pairs={{0,11},{1,10},{2,9},{3,8},{4,15},{5,14},{6,13},{7,12},{8,3},{9,2},... | collective-permute-start | bytes 829448 | tf_op jit(solution)/shard_map/ppermute | solution.py:217
  106.5 31.8 %copy-start.12 = (bf16[360,384]{1,0:T(8,128)(2,1)S(1)}, bf16[360,384]{1,0:T(8,128)(2,1)}, u32[]{:S(2)}) copy-start(bf16[360,384]{1,0:T(8,128)(2,1)} %copy-done.11) | copy-start | bytes 829444
  106.5 21.1 %collective-permute-start.17 = (bf16[360,384]{1,0:T(8,128)(2,1)}, bf16[360,384]{1,0:T(8,128)(2,1)S(1)}, u32[]{:S(2)}, u32[]{:S(2)}) collective-permute-start(bf16[360,384]{1,0:T(8,128)(2,1)} %copy-done.2), channel_id=1, source_target_pairs={{0,12},{1,13},{2,14},{3,15},{4,8},{5,9},{6,10},{7,11},{8,4},{9,5},... | collective-permute-start | bytes 829448 | tf_op jit(solution)/shard_map/ppermute | solution.py:217
  113.4 14.3 %collective-permute-start.18 = (bf16[360,384]{1,0:T(8,128)(2,1)}, bf16[360,384]{1,0:T(8,128)(2,1)S(1)}, u32[]{:S(2)}, u32[]{:S(2)}) collective-permute-start(bf16[360,384]{1,0:T(8,128)(2,1)} %copy-done.1), channel_id=1, source_target_pairs={{0,13},{1,12},{2,15},{3,14},{4,9},{5,8},{6,11},{7,10},{8,5},{9,4},... | collective-permute-start | bytes 829448 | tf_op jit(solution)/shard_map/ppermute | solution.py:217
  115.2 16.3 %collective-permute-start.19 = (bf16[360,384]{1,0:T(8,128)(2,1)}, bf16[360,384]{1,0:T(8,128)(2,1)S(1)}, u32[]{:S(2)}, u32[]{:S(2)}) collective-permute-start(bf16[360,384]{1,0:T(8,128)(2,1)} %copy-done), channel_id=1, source_target_pairs={{0,14},{1,15},{2,12},{3,13},{4,10},{5,11},{6,8},{7,9},{8,6},{9,7},... | collective-permute-start | bytes 829448 | tf_op jit(solution)/shard_map/ppermute | solution.py:217
  121.3 17.0 %collective-permute-start.20 = (bf16[360,384]{1,0:T(8,128)(2,1)S(1)}, bf16[360,384]{1,0:T(8,128)(2,1)S(1)}, u32[]{:S(2)}, u32[]{:S(2)}) collective-permute-start(bf16[360,384]{1,0:T(8,128)(2,1)S(1)} %get-tuple-element.84), channel_id=1, source_target_pairs={{0,15},{1,14},{2,13},{3,12},{4,11},{5,10},{6,9},{7,8},{8,7},{9,6},... | collective-permute-start | bytes 829448 | tf_op jit(solution)/shard_map/ppermute | solution.py:217
  146.6 5.6 %collective-permute-start.25 = (bf16[64,8,2880]{2,1,0:T(8,128)(2,1)S(1)}, bf16[64,8,2880]{2,1,0:T(8,128)(2,1)S(1)}, u32[]{:S(2)}, u32[]{:S(2)}) collective-permute-start(bf16[64,8,2880]{2,1,0:T(8,128)(2,1)S(1)} %get-tuple-element.87), channel_id=1, source_target_pairs={{0,1},{1,0},{2,3},{3,2},{4,5},{5,4},{6,7},{7,6},{8,9},{9,8},{10,11... | collective-permute-start | bytes 8847368 | tf_op jit(solution)/shard_map/ppermute | solution.py:37
  154.2 15.3 %collective-permute-start.26 = (bf16[16,8,2880]{2,1,0:T(8,128)(2,1)S(1)}, bf16[16,8,2880]{2,1,0:T(8,128)(2,1)S(1)}, u32[]{:S(2)}, u32[]{:S(2)}) collective-permute-start(bf16[16,8,2880]{2,1,0:T(8,128)(2,1)S(1)} %get-tuple-element.90), channel_id=1, source_target_pairs={{0,2},{1,17},{2,4},{3,19},{4,6},{5,21},{6,0},{7,23},{8,10},{9,25},... | collective-permute-start | bytes 2211848 | tf_op jit(solution)/shard_map/ppermute | solution.py:37
  154.8 24.3 %collective-permute-start.27 = (bf16[16,8,2880]{2,1,0:T(8,128)(2,1)S(1)}, bf16[16,8,2880]{2,1,0:T(8,128)(2,1)S(1)}, u32[]{:S(2)}, u32[]{:S(2)}) collective-permute-start(bf16[16,8,2880]{2,1,0:T(8,128)(2,1)S(1)} %get-tuple-element.91), channel_id=1, source_target_pairs={{0,4},{1,9},{2,6},{3,11},{4,0},{5,13},{6,2},{7,15},{8,12},{9,1},{1... | collective-permute-start | bytes 2211848 | tf_op jit(solution)/shard_map/ppermute | solution.py:37
  161.4 17.7 %collective-permute-start.28 = (bf16[16,8,2880]{2,1,0:T(8,128)(2,1)S(1)}, bf16[16,8,2880]{2,1,0:T(8,128)(2,1)S(1)}, u32[]{:S(2)}, u32[]{:S(2)}) collective-permute-start(bf16[16,8,2880]{2,1,0:T(8,128)(2,1)S(1)} %get-tuple-element.92), channel_id=1, source_target_pairs={{0,6},{1,25},{2,0},{3,27},{4,2},{5,29},{6,4},{7,31},{8,14},{9,17},... | collective-permute-start | bytes 2211848 | tf_op jit(solution)/shard_map/ppermute | solution.py:37
  179.5 6.9 %collective-permute-start.29 = (bf16[4,8,2880]{2,1,0:T(8,128)(2,1)S(1)}, bf16[4,8,2880]{2,1,0:T(8,128)(2,1)S(1)}, u32[]{:S(2)}, u32[]{:S(2)}) collective-permute-start(bf16[4,8,2880]{2,1,0:T(8,128)(2,1)S(1)} %get-tuple-element.99), channel_id=1, source_target_pairs={{0,16},{1,3},{2,18},{3,5},{4,20},{5,7},{6,22},{7,1},{8,24},{9,11},... | collective-permute-start | bytes 552968 | tf_op jit(solution)/shard_map/ppermute | solution.py:37
  180.2 7.7 %collective-permute-start.31 = (bf16[4,8,2880]{2,1,0:T(8,128)(2,1)S(1)}, bf16[4,8,2880]{2,1,0:T(8,128)(2,1)S(1)}, u32[]{:S(2)}, u32[]{:S(2)}) collective-permute-start(bf16[4,8,2880]{2,1,0:T(8,128)(2,1)S(1)} %get-tuple-element.100), channel_id=1, source_target_pairs={{0,24},{1,7},{2,26},{3,1},{4,28},{5,3},{6,30},{7,5},{8,16},{9,15},... | collective-permute-start | bytes 552968 | tf_op jit(solution)/shard_map/ppermute | solution.py:37
  182.8 7.1 %collective-permute-start.30 = (bf16[4,8,2880]{2,1,0:T(8,128)(2,1)S(1)}, bf16[4,8,2880]{2,1,0:T(8,128)(2,1)S(1)}, u32[]{:S(2)}, u32[]{:S(2)}) collective-permute-start(bf16[4,8,2880]{2,1,0:T(8,128)(2,1)S(1)} %get-tuple-element.101), channel_id=1, source_target_pairs={{0,8},{1,5},{2,10},{3,7},{4,12},{5,1},{6,14},{7,3},{8,0},{9,13},{1... | collective-permute-start | bytes 552968 | tf_op jit(solution)/shard_map/ppermute | solution.py:37
  190.0 6.5 %collective-permute-start.32 = (f32[1,8,2880]{2,1,0:T(8,128)S(1)}, f32[1,8,2880]{2,1,0:T(8,128)S(1)}, u32[]{:S(2)}, u32[]{:S(2)}) collective-permute-start(f32[1,8,2880]{2,1,0:T(8,128)S(1)} %get-tuple-element.102), channel_id=1, source_target_pairs={{0,32},{1,33},{2,34},{3,35},{4,36},{5,37},{6,38},{7,39},{8,40},{9,... | collective-permute-start | bytes 276488 | tf_op jit(solution)/shard_map/ppermute | solution.py:37
  190.1 6.4 %collective-permute-start.34 = (f32[1,8,2880]{2,1,0:T(8,128)S(1)}, f32[1,8,2880]{2,1,0:T(8,128)S(1)}, u32[]{:S(2)}, u32[]{:S(2)}) collective-permute-start(f32[1,8,2880]{2,1,0:T(8,128)S(1)} %get-tuple-element.103), channel_id=1, source_target_pairs={{0,96},{1,97},{2,98},{3,99},{4,100},{5,101},{6,102},{7,103},{8,104... | collective-permute-start | bytes 276488 | tf_op jit(solution)/shard_map/ppermute | solution.py:37
  193.3 6.1 %collective-permute-start.33 = (f32[1,8,2880]{2,1,0:T(8,128)S(1)}, f32[1,8,2880]{2,1,0:T(8,128)S(1)}, u32[]{:S(2)}, u32[]{:S(2)}) collective-permute-start(f32[1,8,2880]{2,1,0:T(8,128)S(1)} %get-tuple-element.104), channel_id=1, source_target_pairs={{0,64},{1,65},{2,66},{3,67},{4,68},{5,69},{6,70},{7,71},{8,72},{9,... | collective-permute-start | bytes 276488 | tf_op jit(solution)/shard_map/ppermute | solution.py:37
where the time goes:
time: 200 us
  waiting for transfers between devices  97.7 us (49%)
  starting transfers between devices  59.2 us (30%)
  Pallas kernels  22.6 us (11%)
  local copies, waits for them, and re-layouts  17.1 us (9%)
  other arithmetic  2.36 us (1%)
    ppermute x20, waiting for transfers between devices, shifted(): return lax.ppermute(a.reshape(-1, 8, a.shape[-1]), BOTH, pairs)  61.9 us
    ppermute x15, waiting for transfers between devices, body(): lax.ppermute(sent[n], 'col', [(i, i ^ n) for i in range(n_col)])  35.9 us
    ppermute x20, starting transfers between devices, shifted(): return lax.ppermute(a.reshape(-1, 8, a.shape[-1]), BOTH, pairs)  31 us
    ppermute x15, starting transfers between devices, body(): lax.ppermute(sent[n], 'col', [(i, i ^ n) for i in range(n_col)])  28.2 us
    unnamed x37, local copies, waits for them, and re-layouts  9.63 us
    pallas_call x1, Pallas kernels, body(): pl.pallas_call(functools.partial(other_kernel, n_col), in_specs=[pl.Block...  8.33 us
    gather x2, local copies, waits for them, and re-layouts, body(): share = jnp.take(share, token, axis=0)  6.29 us
    pallas_call x1, Pallas kernels, body(): pl.pallas_call(functools.partial(turn_kernel, tile_cols), grid_spec=pltpu...  5.37 us
  transfers between devices with their start and end apart: 35, of which 20 were waited for; matrix products, arithmetic and copies ran while one was open for 7% of the time, Pallas kernels for 6%

commit v1 on v0

--- a/solution.py
+++ b/solution.py
@@ -38,7 +38,8 @@
 
 
 def gathered(a, axis):
-    return jnp.concatenate([a.reshape(-1, 8, a.shape[-1])] + [shifted(a, axis, -by) for by in (1, 2, 3)], axis=0)
+    far, near, back = (shifted(a, axis, -by) for by in (2, 1, 3))
+    return jnp.concatenate([a.reshape(-1, 8, a.shape[-1]), near, far, back], axis=0)
 
 
 def turn_kernel(tile_cols, inverse_ref, me_ref, x_ref, *refs):
@@ -273,12 +274,12 @@
             cost_estimate=pl.CostEstimate(flops=2 << 30, bytes_accessed=8 << 20, transcendentals=0),
         )(weights_in)
     )
-    parts = [shifted(parts[by - 1], "first", by).astype(f32) for by in (1, 2, 3)]
+    parts = [shifted(parts[by - 1], "first", by).astype(f32) for by in (2, 1, 3)]
     total = total + parts[0] + parts[1] + parts[2]
     total, gate_out, up_out = lax.optimization_barrier((total, gate_out, up_out))
     for axis, sent_as in (("second", jnp.bfloat16), ("z", f32)):
         total = total.reshape(4, -1, 8, width)
-        parts = [shifted(total[by].astype(sent_as), axis, by).astype(f32) for by in (1, 2, 3)]
+        parts = [shifted(total[by].astype(sent_as), axis, by).astype(f32) for by in (2, 1, 3)]
         total = total[0] + parts[0] + parts[1] + parts[2]
     total = total.reshape(8, width)
     return (gate_out, up_out, total.astype(jnp.bfloat16))

time: 200 us -> 198 us (0.990)
  no operation moved by 1% of the time
where the time goes in v1:
time: 198 us
  waiting for transfers between devices  96.4 us (49%)
  starting transfers between devices  58.1 us (29%)
  Pallas kernels  22.6 us (11%)
  local copies, waits for them, and re-layouts  17.1 us (9%)
  other arithmetic  2.36 us (1%)
    ppermute x20, waiting for transfers between devices, shifted(): return lax.ppermute(a.reshape(-1, 8, a.shape[-1]), BOTH, pairs)  60.5 us
    ppermute x15, waiting for transfers between devices, body(): lax.ppermute(sent[n], 'col', [(i, i ^ n) for i in range(n_col)])  35.9 us
    ppermute x20, starting transfers between devices, shifted(): return lax.ppermute(a.reshape(-1, 8, a.shape[-1]), BOTH, pairs)  29.9 us
    ppermute x15, starting transfers between devices, body(): lax.ppermute(sent[n], 'col', [(i, i ^ n) for i in range(n_col)])  28.2 us
    unnamed x37, local copies, waits for them, and re-layouts  9.63 us
    pallas_call x1, Pallas kernels, body(): pl.pallas_call(functools.partial(other_kernel, n_col), in_specs=[pl.Block...  8.33 us
    gather x2, local copies, waits for them, and re-layouts, body(): share = jnp.take(share, token, axis=0)  6.29 us
    pallas_call x1, Pallas kernels, body(): pl.pallas_call(functools.partial(turn_kernel, tile_cols), grid_spec=pltpu...  5.37 us
  transfers between devices with their start and end apart: 35, of which 20 were waited for; matrix products, arithmetic and copies ran while one was open for 7% of the time, Pallas kernels for 6%

profile of v1, /device:TPU:0, one launch (start us, length us, event | category | flops | bytes accessed | tf_op | source)
XLA Modules:
  0.0 197.6 jit_solution(11321652996733622101)
XLA Ops:
  0.6 1.8 collective-permute-start.2
  2.4 2.9 %collective-permute-start.1 = (bf16[1,8,2880]{2,1,0:T(8,128)(2,1)}, bf16[1,8,2880]{2,1,0:T(8,128)(2,1)S(1)}, u32[]{:S(2)}, u32[]{:S(2)}) collective-permute-start(bf16[1,8,2880]{2,1,0:T(8,128)(2,1)} %bitcast.13), channel_id=1, source_target_pairs={{0,8},{1,5},{2,10},{3,7},{4,12},{5,1},{6,14},{7,3},{8,0},{9,13},{1... | collective-permute-start | bytes 138248 | tf_op jit(solution)/shard_map/ppermute | solution.py:37
  5.3 1.3 collective-permute-start
  6.6 0.8 select_reduce_fusion.inverse_ref
  7.4 2.6 %copy.21.x_ref = bf16[2,180,5760]{2,1,0:T(8,128)(2,1)S(1)} copy(bf16[2,180,5760]{2,0,1:T(2,128)(2,1)} %param.6) | data formatting | bytes 8294400 | tf_op args[0]
  10.1 1.6 collective-permute-start.5
  11.7 2.7 %collective-permute-start.4 = (bf16[4,8,2880]{2,1,0:T(8,128)(2,1)S(1)}, bf16[4,8,2880]{2,1,0:T(8,128)(2,1)S(1)}, u32[]{:S(2)}, u32[]{:S(2)}) collective-permute-start(bf16[4,8,2880]{2,1,0:T(8,128)(2,1)S(1)} %pad_maximum_fusion.1), channel_id=1, source_target_pairs={{0,4},{1,9},{2,6},{3,11},{4,0},{5,13},{6,2},{7,15},{8,12},{9,1},{1... | collective-permute-start | bytes 552968 | tf_op jit(solution)/shard_map/ppermute | solution.py:37
  14.4 1.4 collective-permute-start.3
  15.9 5.4 %turn.1 = (bf16[360,384]{1,0:T(8,128)(2,1)S(1)}, bf16[360,384]{1,0:T(8,128)(2,1)}, bf16[360,384]{1,0:T(8,128)(2,1)}, bf16[360,384]{1,0:T(8,128)(2,1)}, bf16[360,...) custom-call(s32[144]{0:T(256)S(1)} %select_reduce_fusion.inverse_ref, ...), custom_call_target="tpu_custom_call" | custom-call | flops 4294967296 | bytes 16777216 | tf_op jit(solution)/shard_map/turn/pallas_call | solution.py:197
  21.2 0.7 copy-done.5
  21.9 0.7 copy-done.6
  22.6 0.7 copy-done.7
  23.3 0.7 copy-done.8
  24.0 0.7 copy-done.9
  24.8 0.7 copy-done.10
  25.5 0.7 copy-done.11
  26.4 4.1 %collective-permute-start.21 = (bf16[16,8,2880]{2,1,0:T(8,128)(2,1)S(1)}, bf16[16,8,2880]{2,1,0:T(8,128)(2,1)S(1)}, u32[]{:S(2)}, u32[]{:S(2)}) collective-permute-start(bf16[16,8,2880]{2,1,0:T(8,128)(2,1)S(1)} %pad_maximum_fusion), channel_id=1, source_target_pairs={{0,96},{1,97},{2,98},{3,99},{4,100},{5,101},{6,102},{7,103},{8,104... | collective-permute-start | bytes 2211848 | tf_op jit(solution)/shard_map/ppermute | solution.py:37
  30.5 1.3 collective-permute-start.23
  31.8 29.2 %collective-permute-done.21 = bf16[16,8,2880]{2,1,0:T(8,128)(2,1)S(1)} collective-permute-done((bf16[16,8,2880]{2,1,0:T(8,128)(2,1)S(1)}, bf16[16,8,2880]{2,1,0:T(8,128)(2,1)S(1)}, u32[]{:S(2)}, u32[]{:S(2)}) %collective-permute-start.21) | collective-permute-done | bytes 737312 | tf_op jit(solution)/shard_map/ppermute | solution.py:37
  61.3 3.2 %collective-permute-done.23 = bf16[16,8,2880]{2,1,0:T(8,128)(2,1)S(1)} collective-permute-done((bf16[16,8,2880]{2,1,0:T(8,128)(2,1)S(1)}, bf16[16,8,2880]{2,1,0:T(8,128)(2,1)S(1)}, u32[]{:S(2)}, u32[]{:S(2)}) %collective-permute-start.23) | collective-permute-done | bytes 737312 | tf_op jit(solution)/shard_map/ppermute | solution.py:37
  65.2 0.6 collective-permute-start.7
  65.8 0.9 collective-permute-start.8
  66.7 1.3 collective-permute-start.9
  67.9 2.7 %collective-permute-done.6.refs_1_ = bf16[360,384]{1,0:T(8,128)(2,1)} collective-permute-done((bf16[360,384]{1,0:T(8,128)(2,1)}, bf16[360,384]{1,0:T(8,128)(2,1)}, u32[]{:S(2)}, u32[]{:S(2)}) %collective-permute-start.6) | collective-permute-done | bytes 276512 | tf_op jit(solution)/shard_map/ppermute | solution.py:218
  70.9 4.1 %collective-permute-done.7.refs_2_ = bf16[360,384]{1,0:T(8,128)(2,1)} collective-permute-done((bf16[360,384]{1,0:T(8,128)(2,1)}, bf16[360,384]{1,0:T(8,128)(2,1)}, u32[]{:S(2)}, u32[]{:S(2)}) %collective-permute-start.7) | collective-permute-done | bytes 276512 | tf_op jit(solution)/shard_map/ppermute | solution.py:218
  75.0 1.2 collective-permute-start.11
  76.1 3.0 %collective-permute-done.8.refs_3_ = bf16[360,384]{1,0:T(8,128)(2,1)} collective-permute-done((bf16[360,384]{1,0:T(8,128)(2,1)}, bf16[360,384]{1,0:T(8,128)(2,1)}, u32[]{:S(2)}, u32[]{:S(2)}) %collective-permute-start.8) | collective-permute-done | bytes 276512 | tf_op jit(solution)/shard_map/ppermute | solution.py:218
  79.1 2.6 %collective-permute-start.12 = (bf16[360,384]{1,0:T(8,128)(2,1)}, bf16[360,384]{1,0:T(8,128)(2,1)}, u32[]{:S(2)}, u32[]{:S(2)}) collective-permute-start(bf16[360,384]{1,0:T(8,128)(2,1)} %copy-done.7), channel_id=1, source_target_pairs={{0,7},{1,6},{2,5},{3,4},{4,3},{5,2},{6,1},{7,0},{8,15},{9,14},{10,... | collective-permute-start | bytes 829448 | tf_op jit(solution)/shard_map/ppermute | solution.py:218
  81.9 1.0 copy.22
  83.0 4.5 %collective-permute-done.9.refs_4_ = bf16[360,384]{1,0:T(8,128)(2,1)} collective-permute-done((bf16[360,384]{1,0:T(8,128)(2,1)}, bf16[360,384]{1,0:T(8,128)(2,1)}, u32[]{:S(2)}, u32[]{:S(2)}) %collective-permute-start.9) | collective-permute-done | bytes 276512 | tf_op jit(solution)/shard_map/ppermute | solution.py:218
  88.0 3.7 %collective-permute-done.10.refs_5_ = bf16[360,384]{1,0:T(8,128)(2,1)} collective-permute-done((bf16[360,384]{1,0:T(8,128)(2,1)}, bf16[360,384]{1,0:T(8,128)(2,1)}, u32[]{:S(2)}, u32[]{:S(2)}) %collective-permute-start.10) | collective-permute-done | bytes 276512 | tf_op jit(solution)/shard_map/ppermute | solution.py:218
  91.7 0.8 collective-permute-start.14
  92.5 5.2 %collective-permute-done.11.refs_6_ = bf16[360,384]{1,0:T(8,128)(2,1)} collective-permute-done((bf16[360,384]{1,0:T(8,128)(2,1)}, bf16[360,384]{1,0:T(8,128)(2,1)}, u32[]{:S(2)}, u32[]{:S(2)}) %collective-permute-start.11) | collective-permute-done | bytes 276512 | tf_op jit(solution)/shard_map/ppermute | solution.py:218
  97.7 1.0 collective-permute-done.12.refs_7_
  98.7 1.5 collective-permute-start.16
  100.2 5.1 %gather_fusion = f32[1024,2]{1,0:T(8,128)} fusion(f32[1024,2]{1,0:T(8,128)} %copy.22, s32[1024]{0:T(1024)S(1)} %broadcast_clamp_fusion), kind=kCustom, calls=%fused_computation | custom fusion | bytes 20480 | tf_op jit(solution)/shard_map/jit(_take)/gather | solution.py:237
  105.3 1.2 copy.23
  106.5 5.8 %collective-permute-start.17 = (bf16[360,384]{1,0:T(8,128)(2,1)}, bf16[360,384]{1,0:T(8,128)(2,1)S(1)}, u32[]{:S(2)}, u32[]{:S(2)}) collective-permute-start(bf16[360,384]{1,0:T(8,128)(2,1)} %copy-done.2), channel_id=1, source_target_pairs={{0,12},{1,13},{2,14},{3,15},{4,8},{5,9},{6,10},{7,11},{8,4},{9,5},... | collective-permute-start | bytes 829448 | tf_op jit(solution)/shard_map/ppermute | solution.py:218
  112.3 1.1 collective-permute-done.14.refs_9_
  113.4 1.8 collective-permute-start.18
  115.2 6.1 %collective-permute-start.19 = (bf16[360,384]{1,0:T(8,128)(2,1)}, bf16[360,384]{1,0:T(8,128)(2,1)S(1)}, u32[]{:S(2)}, u32[]{:S(2)}) collective-permute-start(bf16[360,384]{1,0:T(8,128)(2,1)} %copy-done), channel_id=1, source_target_pairs={{0,14},{1,15},{2,12},{3,13},{4,10},{5,11},{6,8},{7,9},{8,6},{9,7},... | collective-permute-start | bytes 829448 | tf_op jit(solution)/shard_map/ppermute | solution.py:218
  121.3 4.5 %collective-permute-start.20 = (bf16[360,384]{1,0:T(8,128)(2,1)S(1)}, bf16[360,384]{1,0:T(8,128)(2,1)S(1)}, u32[]{:S(2)}, u32[]{:S(2)}) collective-permute-start(bf16[360,384]{1,0:T(8,128)(2,1)S(1)} %get-tuple-element.84), channel_id=1, source_target_pairs={{0,15},{1,14},{2,13},{3,12},{4,11},{5,10},{6,9},{7,8},{8,7},{9,6},... | collective-permute-start | bytes 829448 | tf_op jit(solution)/shard_map/ppermute | solution.py:218
  125.8 1.8 copy.24.refs_18_.down_ref
  127.7 3.9 %collective-permute-done.19.refs_14_ = bf16[360,384]{1,0:T(8,128)(2,1)S(1)} collective-permute-done((bf16[360,384]{1,0:T(8,128)(2,1)}, bf16[360,384]{1,0:T(8,128)(2,1)S(1)}, u32[]{:S(2)}, u32[]{:S(2)}) %collective-permute-start.19) | collective-permute-done | bytes 276512 | tf_op jit(solution)/shard_map/ppermute | solution.py:218
  131.5 6.7 %collective-permute-done.20.refs_15_ = bf16[360,384]{1,0:T(8,128)(2,1)S(1)} collective-permute-done((bf16[360,384]{1,0:T(8,128)(2,1)S(1)}, bf16[360,384]{1,0:T(8,128)(2,1)S(1)}, u32[]{:S(2)}, u32[]{:S(2)}) %collective-permute-start.20) | collective-permute-done | bytes 276512 | tf_op jit(solution)/shard_map/ppermute | solution.py:218
  138.3 8.3 %other.1 = (bf16[2,360,2880]{2,1,0:T(8,128)(2,1)S(1)}, bf16[64,8,2880]{2,1,0:T(8,128)(2,1)S(1)}) custom-call(s32[1]{0:T(128)} %bitcast.me_ref, bf16[360,384]{1,0:T(8,128)(2,1)S(1)} %copy-done.12, bf16[360,384]{1,0:T(8,128)(2,1)} %collective-permute-done.6.refs_1_, bf16[360,384]{1,0:T(8,128)(2,1)} %collective-permute-done.7.refs_2_, ...), custom_call_target="tpu_custom_call" | custom-call | flops 4294967296 | bytes 16777216 | tf_op jit(solution)/shard_map/other/pallas_call | solution.py:247
  146.7 3.2 %hidden.1.act_ref = bf16[2,512,180]{2,1,0:T(8,128)(2,1)S(1)} custom-call(bf16[2,360,2880]{2,1,0:T(8,128)(2,1)S(1)} %get-tuple-element.93.w_ref, bf16[512,2880]{1,0:T(8,128)(2,1)S(1)} %bitcast.11, f32[2,512]{1,0:T(2,128)S(1)} %get-tuple-element.105.share_ref), custom_call_target="tpu_custom_call" | custom-call | flops 2147483648 | bytes 8388608 | tf_op jit(solution)/shard_map/hidden/pallas_call | solution.py:98
  149.9 2.3 %collective-permute-done.25.came_ref = bf16[64,8,2880]{2,1,0:T(8,128)(2,1)S(1)} collective-permute-done((bf16[64,8,2880]{2,1,0:T(8,128)(2,1)S(1)}, bf16[64,8,2880]{2,1,0:T(8,128)(2,1)S(1)}, u32[]{:S(2)}, u32[]{:S(2)}) %collective-permute-start.25) | collective-permute-done | bytes 2949152 | tf_op jit(solution)/shard_map/ppermute | solution.py:37
  152.2 2.1 %down_own.1 = (f32[16,8,2880]{2,1,0:T(8,128)S(1)}, bf16[16,8,2880]{2,1,0:T(8,128)(2,1)S(1)}, bf16[16,8,2880]{2,1,0:T(8,128)(2,1)S(1)}, bf16[16,8,2880]{2,1,0:T(8,128)(2,1)S(1)}) custom-call(bf16[2,512,180]{2,1,0:T(8,128)(2,1)S(1)} %hidden.1.act_ref, bf16[2,180,2880]{2,1,0:T(8,128)(2,1)S(1)} %copy.24.refs_18_.down_ref, ...), custom_call_target="tpu_custom_call" | custom-call | flops 1073741824 | bytes 8388608 | tf_op jit(solution)/shard_map/down_own/pallas_call | solution.py:170
  154.2 3.3 %collective-permute-start.26 = (bf16[16,8,2880]{2,1,0:T(8,128)(2,1)S(1)}, bf16[16,8,2880]{2,1,0:T(8,128)(2,1)S(1)}, u32[]{:S(2)}, u32[]{:S(2)}) collective-permute-start(bf16[16,8,2880]{2,1,0:T(8,128)(2,1)S(1)} %get-tuple-element.90), channel_id=1, source_target_pairs={{0,4},{1,9},{2,6},{3,11},{4,0},{5,13},{6,2},{7,15},{8,12},{9,1},{1... | collective-permute-start | bytes 2211848 | tf_op jit(solution)/shard_map/ppermute | solution.py:37
  157.5 3.3 %collective-permute-start.27 = (bf16[16,8,2880]{2,1,0:T(8,128)(2,1)S(1)}, bf16[16,8,2880]{2,1,0:T(8,128)(2,1)S(1)}, u32[]{:S(2)}, u32[]{:S(2)}) collective-permute-start(bf16[16,8,2880]{2,1,0:T(8,128)(2,1)S(1)} %get-tuple-element.91), channel_id=1, source_target_pairs={{0,2},{1,17},{2,4},{3,19},{4,6},{5,21},{6,0},{7,23},{8,10},{9,25},... | collective-permute-start | bytes 2211848 | tf_op jit(solution)/shard_map/ppermute | solution.py:37
  160.8 3.7 %emit.1 = (bf16[180,2,2880]{2,1,0:T(2,128)(2,1)}, bf16[180,2,2880]{2,1,0:T(2,128)(2,1)}) custom-call(bf16[2,360,2880]{2,1,0:T(8,128)(2,1)S(1)} %get-tuple-element.93.w_ref), custom_call_target="tpu_custom_call" | custom-call | flops 2147483648 | bytes 8388608 | tf_op jit(solution)/shard_map/emit/pallas_call | solution.py:269
  164.5 3.1 %collective-permute-done.26 = bf16[16,8,2880]{2,1,0:T(8,128)(2,1)S(1)} collective-permute-done((bf16[16,8,2880]{2,1,0:T(8,128)(2,1)S(1)}, bf16[16,8,2880]{2,1,0:T(8,128)(2,1)S(1)}, u32[]{:S(2)}, u32[]{:S(2)}) %collective-permute-start.26) | collective-permute-done | bytes 737312 | tf_op jit(solution)/shard_map/ppermute | solution.py:37
  167.6 8.0 %collective-permute-done.27 = bf16[16,8,2880]{2,1,0:T(8,128)(2,1)S(1)} collective-permute-done((bf16[16,8,2880]{2,1,0:T(8,128)(2,1)S(1)}, bf16[16,8,2880]{2,1,0:T(8,128)(2,1)S(1)}, u32[]{:S(2)}, u32[]{:S(2)}) %collective-permute-start.27) | collective-permute-done | bytes 737312 | tf_op jit(solution)/shard_map/ppermute | solution.py:37
  175.5 3.0 %collective-permute-done.28 = bf16[16,8,2880]{2,1,0:T(8,128)(2,1)S(1)} collective-permute-done((bf16[16,8,2880]{2,1,0:T(8,128)(2,1)S(1)}, bf16[16,8,2880]{2,1,0:T(8,128)(2,1)S(1)}, u32[]{:S(2)}, u32[]{:S(2)}) %collective-permute-start.28) | collective-permute-done | bytes 737312 | tf_op jit(solution)/shard_map/ppermute | solution.py:37
  179.0 3.3 %collective-permute-start.31 = (bf16[4,8,2880]{2,1,0:T(8,128)(2,1)S(1)}, bf16[4,8,2880]{2,1,0:T(8,128)(2,1)S(1)}, u32[]{:S(2)}, u32[]{:S(2)}) collective-permute-start(bf16[4,8,2880]{2,1,0:T(8,128)(2,1)S(1)} %get-tuple-element.100), channel_id=1, source_target_pairs={{0,24},{1,7},{2,26},{3,1},{4,28},{5,3},{6,30},{7,5},{8,16},{9,15},... | collective-permute-start | bytes 552968 | tf_op jit(solution)/shard_map/ppermute | solution.py:37
  182.4 3.7 %collective-permute-done.29 = bf16[4,8,2880]{2,1,0:T(8,128)(2,1)S(1)} collective-permute-done((bf16[4,8,2880]{2,1,0:T(8,128)(2,1)S(1)}, bf16[4,8,2880]{2,1,0:T(8,128)(2,1)S(1)}, u32[]{:S(2)}, u32[]{:S(2)}) %collective-permute-start.29) | collective-permute-done | bytes 184352 | tf_op jit(solution)/shard_map/ppermute | solution.py:37
  186.1 3.0 %collective-permute-done.30 = bf16[4,8,2880]{2,1,0:T(8,128)(2,1)S(1)} collective-permute-done((bf16[4,8,2880]{2,1,0:T(8,128)(2,1)S(1)}, bf16[4,8,2880]{2,1,0:T(8,128)(2,1)S(1)}, u32[]{:S(2)}, u32[]{:S(2)}) %collective-permute-start.30) | collective-permute-done | bytes 184352 | tf_op jit(solution)/shard_map/ppermute | solution.py:37
  189.3 0.7 collective-permute-start.32
  189.9 1.2 collective-permute-start.34
  191.1 0.8 collective-permute-start.33
  192.0 3.5 %collective-permute-done.32 = f32[1,8,2880]{2,1,0:T(8,128)S(1)} collective-permute-done((f32[1,8,2880]{2,1,0:T(8,128)S(1)}, f32[1,8,2880]{2,1,0:T(8,128)S(1)}, u32[]{:S(2)}, u32[]{:S(2)}) %collective-permute-start.32) | collective-permute-done | bytes 92192 | tf_op jit(solution)/shard_map/ppermute | solution.py:37
  195.4 1.5 collective-permute-done.33
  196.9 0.7 fusion.3
  (70 shorter events, 2.9 us)
Async XLA Ops:
  0.6 9.4 %collective-permute-start.2 = (bf16[1,8,2880]{2,1,0:T(8,128)(2,1)}, bf16[1,8,2880]{2,1,0:T(8,128)(2,1)S(1)}, u32[]{:S(2)}, u32[]{:S(2)}) collective-permute-start(bf16[1,8,2880]{2,1,0:T(8,128)(2,1)} %bitcast.12), channel_id=1, source_target_pairs={{0,16},{1,3},{2,18},{3,5},{4,20},{5,7},{6,22},{7,1},{8,24},{9,11},... | collective-permute-start | bytes 138248 | tf_op jit(solution)/shard_map/ppermute | solution.py:37
  2.4 7.7 %collective-permute-start.1 = (bf16[1,8,2880]{2,1,0:T(8,128)(2,1)}, bf16[1,8,2880]{2,1,0:T(8,128)(2,1)S(1)}, u32[]{:S(2)}, u32[]{:S(2)}) collective-permute-start(bf16[1,8,2880]{2,1,0:T(8,128)(2,1)} %bitcast.13), channel_id=1, source_target_pairs={{0,8},{1,5},{2,10},{3,7},{4,12},{5,1},{6,14},{7,3},{8,0},{9,13},{1... | collective-permute-start | bytes 138248 | tf_op jit(solution)/shard_map/ppermute | solution.py:37
  5.3 4.8 %collective-permute-start = (bf16[1,8,2880]{2,1,0:T(8,128)(2,1)}, bf16[1,8,2880]{2,1,0:T(8,128)(2,1)S(1)}, u32[]{:S(2)}, u32[]{:S(2)}) collective-permute-start(bf16[1,8,2880]{2,1,0:T(8,128)(2,1)} %bitcast.14), channel_id=1, source_target_pairs={{0,24},{1,7},{2,26},{3,1},{4,28},{5,3},{6,30},{7,5},{8,16},{9,15},... | collective-permute-start | bytes 138248 | tf_op jit(solution)/shard_map/ppermute | solution.py:37
  7.4 2.7 %copy-start.14 = (bf16[8,2880]{1,0:T(8,128)(2,1)S(1)}, bf16[8,2880]{1,0:T(8,128)(2,1)}, u32[]{:S(2)}) copy-start(bf16[8,2880]{1,0:T(8,128)(2,1)} %param.9) | copy-start | bytes 138244
  10.1 16.1 %collective-permute-start.5 = (bf16[4,8,2880]{2,1,0:T(8,128)(2,1)S(1)}, bf16[4,8,2880]{2,1,0:T(8,128)(2,1)S(1)}, u32[]{:S(2)}, u32[]{:S(2)}) collective-permute-start(bf16[4,8,2880]{2,1,0:T(8,128)(2,1)S(1)} %pad_maximum_fusion.1), channel_id=1, source_target_pairs={{0,2},{1,17},{2,4},{3,19},{4,6},{5,21},{6,0},{7,23},{8,10},{9,25},... | collective-permute-start | bytes 552968 | tf_op jit(solution)/shard_map/ppermute | solution.py:37
  11.7 14.5 %collective-permute-start.4 = (bf16[4,8,2880]{2,1,0:T(8,128)(2,1)S(1)}, bf16[4,8,2880]{2,1,0:T(8,128)(2,1)S(1)}, u32[]{:S(2)}, u32[]{:S(2)}) collective-permute-start(bf16[4,8,2880]{2,1,0:T(8,128)(2,1)S(1)} %pad_maximum_fusion.1), channel_id=1, source_target_pairs={{0,4},{1,9},{2,6},{3,11},{4,0},{5,13},{6,2},{7,15},{8,12},{9,1},{1... | collective-permute-start | bytes 552968 | tf_op jit(solution)/shard_map/ppermute | solution.py:37
  14.4 11.8 %collective-permute-start.3 = (bf16[4,8,2880]{2,1,0:T(8,128)(2,1)S(1)}, bf16[4,8,2880]{2,1,0:T(8,128)(2,1)S(1)}, u32[]{:S(2)}, u32[]{:S(2)}) collective-permute-start(bf16[4,8,2880]{2,1,0:T(8,128)(2,1)S(1)} %pad_maximum_fusion.1), channel_id=1, source_target_pairs={{0,6},{1,25},{2,0},{3,27},{4,2},{5,29},{6,4},{7,31},{8,14},{9,17},... | collective-permute-start | bytes 552968 | tf_op jit(solution)/shard_map/ppermute | solution.py:37
  21.2 0.7 copy-start.5
  21.9 0.7 copy-start.6
  22.6 0.7 copy-start.7
  23.3 0.7 copy-start.8
  24.0 0.7 copy-start.9
  24.8 0.7 copy-start.10
  25.5 0.7 copy-start.11
  26.2 35.1 %copy-start = (bf16[360,384]{1,0:T(8,128)(2,1)}, bf16[360,384]{1,0:T(8,128)(2,1)S(1)}, u32[]{:S(2)}) copy-start(bf16[360,384]{1,0:T(8,128)(2,1)S(1)} %get-tuple-element.83) | copy-start | bytes 829444
  26.2 35.1 %copy-start.1 = (bf16[360,384]{1,0:T(8,128)(2,1)}, bf16[360,384]{1,0:T(8,128)(2,1)S(1)}, u32[]{:S(2)}) copy-start(bf16[360,384]{1,0:T(8,128)(2,1)S(1)} %get-tuple-element.82) | copy-start | bytes 829444
  26.2 35.1 %copy-start.2 = (bf16[360,384]{1,0:T(8,128)(2,1)}, bf16[360,384]{1,0:T(8,128)(2,1)S(1)}, u32[]{:S(2)}) copy-start(bf16[360,384]{1,0:T(8,128)(2,1)S(1)} %get-tuple-element.81) | copy-start | bytes 829444
  26.2 35.1 %copy-start.3 = (bf16[360,384]{1,0:T(8,128)(2,1)}, bf16[360,384]{1,0:T(8,128)(2,1)S(1)}, u32[]{:S(2)}) copy-start(bf16[360,384]{1,0:T(8,128)(2,1)S(1)} %get-tuple-element.80) | copy-start | bytes 829444
  26.2 35.1 %copy-start.4 = (bf16[360,384]{1,0:T(8,128)(2,1)}, bf16[360,384]{1,0:T(8,128)(2,1)S(1)}, u32[]{:S(2)}) copy-start(bf16[360,384]{1,0:T(8,128)(2,1)S(1)} %get-tuple-element.79) | copy-start | bytes 829444
  26.4 40.2 %copy-start.13 = (f32[1024,4]{0,1:T(4,128)S(1)}, f32[1024,4]{0,1:T(4,128)}, u32[]{:S(2)}) copy-start(f32[1024,4]{0,1:T(4,128)} %param.11) | copy-start | bytes 49156
  26.4 55.4 %copy-start.15 = (s32[1024,4]{0,1:T(4,128)S(1)}, s32[1024,4]{0,1:T(4,128)}, u32[]{:S(2)}) copy-start(s32[1024,4]{0,1:T(4,128)} %param.10) | copy-start | bytes 49156
  26.4 34.7 %collective-permute-start.21 = (bf16[16,8,2880]{2,1,0:T(8,128)(2,1)S(1)}, bf16[16,8,2880]{2,1,0:T(8,128)(2,1)S(1)}, u32[]{:S(2)}, u32[]{:S(2)}) collective-permute-start(bf16[16,8,2880]{2,1,0:T(8,128)(2,1)S(1)} %pad_maximum_fusion), channel_id=1, source_target_pairs={{0,96},{1,97},{2,98},{3,99},{4,100},{5,101},{6,102},{7,103},{8,104... | collective-permute-start | bytes 2211848 | tf_op jit(solution)/shard_map/ppermute | solution.py:37
  30.5 30.7 %collective-permute-start.22 = (bf16[16,8,2880]{2,1,0:T(8,128)(2,1)S(1)}, bf16[16,8,2880]{2,1,0:T(8,128)(2,1)S(1)}, u32[]{:S(2)}, u32[]{:S(2)}) collective-permute-start(bf16[16,8,2880]{2,1,0:T(8,128)(2,1)S(1)} %pad_maximum_fusion), channel_id=1, source_target_pairs={{0,64},{1,65},{2,66},{3,67},{4,68},{5,69},{6,70},{7,71},{8,72},{9,... | collective-permute-start | bytes 2211848 | tf_op jit(solution)/shard_map/ppermute | solution.py:37
  30.5 34.0 %collective-permute-start.23 = (bf16[16,8,2880]{2,1,0:T(8,128)(2,1)S(1)}, bf16[16,8,2880]{2,1,0:T(8,128)(2,1)S(1)}, u32[]{:S(2)}, u32[]{:S(2)}) collective-permute-start(bf16[16,8,2880]{2,1,0:T(8,128)(2,1)S(1)} %pad_maximum_fusion), channel_id=1, source_target_pairs={{0,32},{1,33},{2,34},{3,35},{4,36},{5,37},{6,38},{7,39},{8,40},{9,... | collective-permute-start | bytes 2211848 | tf_op jit(solution)/shard_map/ppermute | solution.py:37
  64.6 73.7 %collective-permute-start.24 = (bf16[64,8,2880]{2,1,0:T(8,128)(2,1)S(1)}, bf16[64,8,2880]{2,1,0:T(8,128)(2,1)}, u32[]{:S(2)}, u32[]{:S(2)}) collective-permute-start(bf16[64,8,2880]{2,1,0:T(8,128)(2,1)S(1)} %constant_dynamic-update-slice_fusion), channel_id=1, source_target_pairs={{0,1},{1,0},{2,3},{3,2},{4,5},{5,4},{6,7},{7,6},{8,9},{9,8},{10,11... | collective-permute-start | bytes 8847368 | tf_op jit(solution)/shard_map/ppermute | solution.py:37
  64.7 6.0 %collective-permute-start.6 = (bf16[360,384]{1,0:T(8,128)(2,1)}, bf16[360,384]{1,0:T(8,128)(2,1)}, u32[]{:S(2)}, u32[]{:S(2)}) collective-permute-start(bf16[360,384]{1,0:T(8,128)(2,1)} %get-tuple-element.70), channel_id=1, source_target_pairs={{0,1},{1,0},{2,3},{3,2},{4,5},{5,4},{6,7},{7,6},{8,9},{9,8},{10,11... | collective-permute-start | bytes 829448 | tf_op jit(solution)/shard_map/ppermute | solution.py:218
  65.2 9.8 %collective-permute-start.7 = (bf16[360,384]{1,0:T(8,128)(2,1)}, bf16[360,384]{1,0:T(8,128)(2,1)}, u32[]{:S(2)}, u32[]{:S(2)}) collective-permute-start(bf16[360,384]{1,0:T(8,128)(2,1)} %get-tuple-element.71), channel_id=1, source_target_pairs={{0,2},{1,3},{2,0},{3,1},{4,6},{5,7},{6,4},{7,5},{8,10},{9,11},{10,... | collective-permute-start | bytes 829448 | tf_op jit(solution)/shard_map/ppermute | solution.py:218
  65.8 13.4 %collective-permute-start.8 = (bf16[360,384]{1,0:T(8,128)(2,1)}, bf16[360,384]{1,0:T(8,128)(2,1)}, u32[]{:S(2)}, u32[]{:S(2)}) collective-permute-start(bf16[360,384]{1,0:T(8,128)(2,1)} %get-tuple-element.72), channel_id=1, source_target_pairs={{0,3},{1,2},{2,1},{3,0},{4,7},{5,6},{6,5},{7,4},{8,11},{9,10},{10,... | collective-permute-start | bytes 829448 | tf_op jit(solution)/shard_map/ppermute | solution.py:218
  66.7 20.9 %collective-permute-start.9 = (bf16[360,384]{1,0:T(8,128)(2,1)}, bf16[360,384]{1,0:T(8,128)(2,1)}, u32[]{:S(2)}, u32[]{:S(2)}) collective-permute-start(bf16[360,384]{1,0:T(8,128)(2,1)} %copy-done.10), channel_id=1, source_target_pairs={{0,4},{1,5},{2,6},{3,7},{4,0},{5,1},{6,2},{7,3},{8,12},{9,13},{10,... | collective-permute-start | bytes 829448 | tf_op jit(solution)/shard_map/ppermute | solution.py:218
  70.7 21.0 %collective-permute-start.10 = (bf16[360,384]{1,0:T(8,128)(2,1)}, bf16[360,384]{1,0:T(8,128)(2,1)}, u32[]{:S(2)}, u32[]{:S(2)}) collective-permute-start(bf16[360,384]{1,0:T(8,128)(2,1)} %copy-done.9), channel_id=1, source_target_pairs={{0,5},{1,4},{2,7},{3,6},{4,1},{5,0},{6,3},{7,2},{8,13},{9,12},{10,... | collective-permute-start | bytes 829448 | tf_op jit(solution)/shard_map/ppermute | solution.py:218
  75.0 22.7 %collective-permute-start.11 = (bf16[360,384]{1,0:T(8,128)(2,1)}, bf16[360,384]{1,0:T(8,128)(2,1)}, u32[]{:S(2)}, u32[]{:S(2)}) collective-permute-start(bf16[360,384]{1,0:T(8,128)(2,1)} %copy-done.8), channel_id=1, source_target_pairs={{0,6},{1,7},{2,4},{3,5},{4,2},{5,3},{6,0},{7,1},{8,14},{9,15},{10,... | collective-permute-start | bytes 829448 | tf_op jit(solution)/shard_map/ppermute | solution.py:218
  79.1 19.6 %collective-permute-start.12 = (bf16[360,384]{1,0:T(8,128)(2,1)}, bf16[360,384]{1,0:T(8,128)(2,1)}, u32[]{:S(2)}, u32[]{:S(2)}) collective-permute-start(bf16[360,384]{1,0:T(8,128)(2,1)} %copy-done.7), channel_id=1, source_target_pairs={{0,7},{1,6},{2,5},{3,4},{4,3},{5,2},{6,1},{7,0},{8,15},{9,14},{10,... | collective-permute-start | bytes 829448 | tf_op jit(solution)/shard_map/ppermute | solution.py:218
  87.5 19.0 %collective-permute-start.13 = (bf16[360,384]{1,0:T(8,128)(2,1)}, bf16[360,384]{1,0:T(8,128)(2,1)}, u32[]{:S(2)}, u32[]{:S(2)}) collective-permute-start(bf16[360,384]{1,0:T(8,128)(2,1)} %copy-done.6), channel_id=1, source_target_pairs={{0,8},{1,9},{2,10},{3,11},{4,12},{5,13},{6,14},{7,15},{8,0},{9,1},... | collective-permute-start | bytes 829448 | tf_op jit(solution)/shard_map/ppermute | solution.py:218
  91.7 21.7 %collective-permute-start.14 = (bf16[360,384]{1,0:T(8,128)(2,1)}, bf16[360,384]{1,0:T(8,128)(2,1)}, u32[]{:S(2)}, u32[]{:S(2)}) collective-permute-start(bf16[360,384]{1,0:T(8,128)(2,1)} %copy-done.5), channel_id=1, source_target_pairs={{0,9},{1,8},{2,11},{3,10},{4,13},{5,12},{6,15},{7,14},{8,1},{9,0},... | collective-permute-start | bytes 829448 | tf_op jit(solution)/shard_map/ppermute | solution.py:218
  97.7 17.5 %collective-permute-start.15 = (bf16[360,384]{1,0:T(8,128)(2,1)}, bf16[360,384]{1,0:T(8,128)(2,1)}, u32[]{:S(2)}, u32[]{:S(2)}) collective-permute-start(bf16[360,384]{1,0:T(8,128)(2,1)} %copy-done.4), channel_id=1, source_target_pairs={{0,10},{1,11},{2,8},{3,9},{4,14},{5,15},{6,12},{7,13},{8,2},{9,3},... | collective-permute-start | bytes 829448 | tf_op jit(solution)/shard_map/ppermute | solution.py:218
  98.7 22.6 %collective-permute-start.16 = (bf16[360,384]{1,0:T(8,128)(2,1)}, bf16[360,384]{1,0:T(8,128)(2,1)}, u32[]{:S(2)}, u32[]{:S(2)}) collective-permute-start(bf16[360,384]{1,0:T(8,128)(2,1)} %copy-done.3), channel_id=1, source_target_pairs={{0,11},{1,10},{2,9},{3,8},{4,15},{5,14},{6,13},{7,12},{8,3},{9,2},... | collective-permute-start | bytes 829448 | tf_op jit(solution)/shard_map/ppermute | solution.py:218
  106.5 31.8 %copy-start.12 = (bf16[360,384]{1,0:T(8,128)(2,1)S(1)}, bf16[360,384]{1,0:T(8,128)(2,1)}, u32[]{:S(2)}) copy-start(bf16[360,384]{1,0:T(8,128)(2,1)} %copy-done.11) | copy-start | bytes 829444
  106.5 21.1 %collective-permute-start.17 = (bf16[360,384]{1,0:T(8,128)(2,1)}, bf16[360,384]{1,0:T(8,128)(2,1)S(1)}, u32[]{:S(2)}, u32[]{:S(2)}) collective-permute-start(bf16[360,384]{1,0:T(8,128)(2,1)} %copy-done.2), channel_id=1, source_target_pairs={{0,12},{1,13},{2,14},{3,15},{4,8},{5,9},{6,10},{7,11},{8,4},{9,5},... | collective-permute-start | bytes 829448 | tf_op jit(solution)/shard_map/ppermute | solution.py:218
  113.4 14.3 %collective-permute-start.18 = (bf16[360,384]{1,0:T(8,128)(2,1)}, bf16[360,384]{1,0:T(8,128)(2,1)S(1)}, u32[]{:S(2)}, u32[]{:S(2)}) collective-permute-start(bf16[360,384]{1,0:T(8,128)(2,1)} %copy-done.1), channel_id=1, source_target_pairs={{0,13},{1,12},{2,15},{3,14},{4,9},{5,8},{6,11},{7,10},{8,5},{9,4},... | collective-permute-start | bytes 829448 | tf_op jit(solution)/shard_map/ppermute | solution.py:218
  115.2 16.3 %collective-permute-start.19 = (bf16[360,384]{1,0:T(8,128)(2,1)}, bf16[360,384]{1,0:T(8,128)(2,1)S(1)}, u32[]{:S(2)}, u32[]{:S(2)}) collective-permute-start(bf16[360,384]{1,0:T(8,128)(2,1)} %copy-done), channel_id=1, source_target_pairs={{0,14},{1,15},{2,12},{3,13},{4,10},{5,11},{6,8},{7,9},{8,6},{9,7},... | collective-permute-start | bytes 829448 | tf_op jit(solution)/shard_map/ppermute | solution.py:218
  121.3 17.0 %collective-permute-start.20 = (bf16[360,384]{1,0:T(8,128)(2,1)S(1)}, bf16[360,384]{1,0:T(8,128)(2,1)S(1)}, u32[]{:S(2)}, u32[]{:S(2)}) collective-permute-start(bf16[360,384]{1,0:T(8,128)(2,1)S(1)} %get-tuple-element.84), channel_id=1, source_target_pairs={{0,15},{1,14},{2,13},{3,12},{4,11},{5,10},{6,9},{7,8},{8,7},{9,6},... | collective-permute-start | bytes 829448 | tf_op jit(solution)/shard_map/ppermute | solution.py:218
  146.6 5.6 %collective-permute-start.25 = (bf16[64,8,2880]{2,1,0:T(8,128)(2,1)S(1)}, bf16[64,8,2880]{2,1,0:T(8,128)(2,1)S(1)}, u32[]{:S(2)}, u32[]{:S(2)}) collective-permute-start(bf16[64,8,2880]{2,1,0:T(8,128)(2,1)S(1)} %get-tuple-element.87), channel_id=1, source_target_pairs={{0,1},{1,0},{2,3},{3,2},{4,5},{5,4},{6,7},{7,6},{8,9},{9,8},{10,11... | collective-permute-start | bytes 8847368 | tf_op jit(solution)/shard_map/ppermute | solution.py:37
  154.2 13.3 %collective-permute-start.26 = (bf16[16,8,2880]{2,1,0:T(8,128)(2,1)S(1)}, bf16[16,8,2880]{2,1,0:T(8,128)(2,1)S(1)}, u32[]{:S(2)}, u32[]{:S(2)}) collective-permute-start(bf16[16,8,2880]{2,1,0:T(8,128)(2,1)S(1)} %get-tuple-element.90), channel_id=1, source_target_pairs={{0,4},{1,9},{2,6},{3,11},{4,0},{5,13},{6,2},{7,15},{8,12},{9,1},{1... | collective-permute-start | bytes 2211848 | tf_op jit(solution)/shard_map/ppermute | solution.py:37
  157.5 18.0 %collective-permute-start.27 = (bf16[16,8,2880]{2,1,0:T(8,128)(2,1)S(1)}, bf16[16,8,2880]{2,1,0:T(8,128)(2,1)S(1)}, u32[]{:S(2)}, u32[]{:S(2)}) collective-permute-start(bf16[16,8,2880]{2,1,0:T(8,128)(2,1)S(1)} %get-tuple-element.91), channel_id=1, source_target_pairs={{0,2},{1,17},{2,4},{3,19},{4,6},{5,21},{6,0},{7,23},{8,10},{9,25},... | collective-permute-start | bytes 2211848 | tf_op jit(solution)/shard_map/ppermute | solution.py:37
  160.8 17.7 %collective-permute-start.28 = (bf16[16,8,2880]{2,1,0:T(8,128)(2,1)S(1)}, bf16[16,8,2880]{2,1,0:T(8,128)(2,1)S(1)}, u32[]{:S(2)}, u32[]{:S(2)}) collective-permute-start(bf16[16,8,2880]{2,1,0:T(8,128)(2,1)S(1)} %get-tuple-element.92), channel_id=1, source_target_pairs={{0,6},{1,25},{2,0},{3,27},{4,2},{5,29},{6,4},{7,31},{8,14},{9,17},... | collective-permute-start | bytes 2211848 | tf_op jit(solution)/shard_map/ppermute | solution.py:37
  179.0 7.2 %collective-permute-start.29 = (bf16[4,8,2880]{2,1,0:T(8,128)(2,1)S(1)}, bf16[4,8,2880]{2,1,0:T(8,128)(2,1)S(1)}, u32[]{:S(2)}, u32[]{:S(2)}) collective-permute-start(bf16[4,8,2880]{2,1,0:T(8,128)(2,1)S(1)} %get-tuple-element.99), channel_id=1, source_target_pairs={{0,8},{1,5},{2,10},{3,7},{4,12},{5,1},{6,14},{7,3},{8,0},{9,13},{1... | collective-permute-start | bytes 552968 | tf_op jit(solution)/shard_map/ppermute | solution.py:37
  179.0 7.1 %collective-permute-start.31 = (bf16[4,8,2880]{2,1,0:T(8,128)(2,1)S(1)}, bf16[4,8,2880]{2,1,0:T(8,128)(2,1)S(1)}, u32[]{:S(2)}, u32[]{:S(2)}) collective-permute-start(bf16[4,8,2880]{2,1,0:T(8,128)(2,1)S(1)} %get-tuple-element.100), channel_id=1, source_target_pairs={{0,24},{1,7},{2,26},{3,1},{4,28},{5,3},{6,30},{7,5},{8,16},{9,15},... | collective-permute-start | bytes 552968 | tf_op jit(solution)/shard_map/ppermute | solution.py:37
  182.4 6.8 %collective-permute-start.30 = (bf16[4,8,2880]{2,1,0:T(8,128)(2,1)S(1)}, bf16[4,8,2880]{2,1,0:T(8,128)(2,1)S(1)}, u32[]{:S(2)}, u32[]{:S(2)}) collective-permute-start(bf16[4,8,2880]{2,1,0:T(8,128)(2,1)S(1)} %get-tuple-element.101), channel_id=1, source_target_pairs={{0,16},{1,3},{2,18},{3,5},{4,20},{5,7},{6,22},{7,1},{8,24},{9,11},... | collective-permute-start | bytes 552968 | tf_op jit(solution)/shard_map/ppermute | solution.py:37
  189.3 6.2 %collective-permute-start.32 = (f32[1,8,2880]{2,1,0:T(8,128)S(1)}, f32[1,8,2880]{2,1,0:T(8,128)S(1)}, u32[]{:S(2)}, u32[]{:S(2)}) collective-permute-start(f32[1,8,2880]{2,1,0:T(8,128)S(1)} %get-tuple-element.102), channel_id=1, source_target_pairs={{0,64},{1,65},{2,66},{3,67},{4,68},{5,69},{6,70},{7,71},{8,72},{9,... | collective-permute-start | bytes 276488 | tf_op jit(solution)/shard_map/ppermute | solution.py:37
  189.9 5.5 %collective-permute-start.34 = (f32[1,8,2880]{2,1,0:T(8,128)S(1)}, f32[1,8,2880]{2,1,0:T(8,128)S(1)}, u32[]{:S(2)}, u32[]{:S(2)}) collective-permute-start(f32[1,8,2880]{2,1,0:T(8,128)S(1)} %get-tuple-element.103), channel_id=1, source_target_pairs={{0,96},{1,97},{2,98},{3,99},{4,100},{5,101},{6,102},{7,103},{8,104... | collective-permute-start | bytes 276488 | tf_op jit(solution)/shard_map/ppermute | solution.py:37
  191.1 5.8 %collective-permute-start.33 = (f32[1,8,2880]{2,1,0:T(8,128)S(1)}, f32[1,8,2880]{2,1,0:T(8,128)S(1)}, u32[]{:S(2)}, u32[]{:S(2)}) collective-permute-start(f32[1,8,2880]{2,1,0:T(8,128)S(1)} %get-tuple-element.104), channel_id=1, source_target_pairs={{0,32},{1,33},{2,34},{3,35},{4,36},{5,37},{6,38},{7,39},{8,40},{9,... | collective-permute-start | bytes 276488 | tf_op jit(solution)/shard_map/ppermute | solution.py:37
